TPU v7x, 32 devices: a whole 2x2x4 slice. The times are simulated.
32 devices in a mesh: row: 8 (over y, x, core), col: 4 (over z).
Axes of the slice: x: 2, y: 2, z: 4, core: 2. Of those that a mesh axis runs over, the one named last changes fastest.
Arguments:
- grad_out: bfloat16 [256, 128, 320], P('row', 'col'), may hold values from -0.078125 to 0.078125
- dec_pre: bfloat16 [256, 128, 320], P('row', 'col'), may hold values from -6 to 6
- ctrl_out: bfloat16 [256, 128, 320], P('row', 'col'), may hold values from -6 to 6
- ctrl_mid: bfloat16 [256, 128, 320], P('row', 'col'), may hold values from -6 to 6
- ctrl_in: bfloat16 [256, 128, 320], P('row', 'col'), may hold values from -6 to 6
- dec_weight: bfloat16 [3, 3, 320, 320], replicated, may hold values from -0.109375 to 0.109375
- zero_weight: bfloat16 [320, 320], replicated, may hold values from -0.3125 to 0.3125
- ctrl_weight: bfloat16 [3, 3, 320, 320], replicated, may hold values from -0.109375 to 0.109375
Outputs:
- grad_zero: float32 [320, 320], P('row', 'col')
- grad_ctrl: float32 [3, 3, 320, 320], P(None, None, 'row', 'col')
- grad_in: float32 [3, 3, 320, 320], P(None, None, 'row', 'col')
All inputs are finite; a program needn't handle non-finite values.
Results may differ from a plain program's by a relative error of at most 0.024.
Values may be sent and summed in bfloat16 or wider, within the bound.
No kernel may reach another device: no remote copies, remote signals or barrier semaphores. Data moves between devices by JAX's collectives and lax.ppermute only.
A program may use at most 128 MiB of HBM per device.

v0:
```python
import jax
import jax.numpy as jnp
from jax import lax
from jax.sharding import PartitionSpec as P


def with_halo(cells, sides, width):
    for axis, dim in sides:
        count = lax.axis_size(axis)
        ends = count - 1
        head = lax.slice_in_dim(cells, 0, width, axis=dim)
        tail = lax.slice_in_dim(cells, cells.shape[dim] - width, cells.shape[dim], axis=dim)
        cells = jnp.concatenate(
            [
                lax.ppermute(tail, axis, [(i, (i + 1) % count) for i in range(ends)]),
                cells,
                lax.ppermute(head, axis, [((i + 1) % count, i) for i in range(ends)]),
            ],
            axis=dim,
        )
    return cells


def silu_slope(values):
    sigm = jax.nn.sigmoid(values)
    return sigm * (1.0 + values * (1.0 - sigm))


def transpose_local(padded, kernel, height, breadth):
    channels = padded.shape[2]
    summed = jnp.zeros((height * breadth, kernel.shape[2]), jnp.float32)
    for tap_row in range(3):
        for tap_col in range(3):
            window = padded[
                2 - tap_row : 2 - tap_row + height, 2 - tap_col : 2 - tap_col + breadth
            ].reshape(-1, channels)
            summed = summed + lax.dot_general(
                window,
                kernel[tap_row, tap_col],
                (((1,), (1,)), ((), ())),
                preferred_element_type=jnp.float32,
            )
    return summed.reshape(height, breadth, -1)


def weight_local(padded, cotangent):
    height, breadth, channels = cotangent.shape
    flat_grad = cotangent.reshape(-1, channels)
    taps = []
    for tap_row in range(3):
        for tap_col in range(3):
            window = padded[tap_row : tap_row + height, tap_col : tap_col + breadth].reshape(
                -1, padded.shape[2]
            )
            taps.append(
                lax.dot_general(
                    window, flat_grad, (((0,), (0,)), ((), ())), preferred_element_type=jnp.float32
                )
            )
    return jnp.stack(taps)


def on_device(grad_out, dec_pre, ctrl_out, ctrl_mid, ctrl_in, dec_weight, zero_weight, ctrl_weight):
    height, breadth, channels = grad_out.shape
    grad_pad = with_halo(grad_out, (("row", 0), ("col", 1)), 1)
    activations = jnp.concatenate(
        [jax.nn.silu(ctrl_mid.astype(jnp.float32)), jax.nn.silu(ctrl_in.astype(jnp.float32))],
        axis=2,
    ).astype(jnp.bfloat16)
    act_pad = with_halo(activations, (("row", 0), ("col", 1)), 1)
    dec_grad = (
        silu_slope(dec_pre.astype(jnp.float32))
        * transpose_local(grad_pad, dec_weight, height, breadth)
    ).astype(jnp.bfloat16)
    flat_dec = dec_grad.reshape(-1, channels)
    zero_part = lax.dot_general(
        ctrl_out.reshape(-1, channels),
        flat_dec,
        (((0,), (0,)), ((), ())),
        preferred_element_type=jnp.float32,
    )
    ctrl_grad = (
        lax.dot_general(
            flat_dec, zero_weight, (((1,), (1,)), ((), ())), preferred_element_type=jnp.float32
        )
        .astype(jnp.bfloat16)
        .reshape(height, breadth, channels)
    )
    ctrl_pad = with_halo(ctrl_grad, (("row", 0), ("col", 1)), 1)
    mid_grad = (
        silu_slope(ctrl_mid.astype(jnp.float32))
        * transpose_local(ctrl_pad, ctrl_weight, height, breadth)
    ).astype(jnp.bfloat16)
    ctrl_part = weight_local(act_pad[:, :, :channels], ctrl_grad)
    input_part = weight_local(act_pad[:, :, channels:], mid_grad)
    stacked = jnp.concatenate([zero_part[None], ctrl_part, input_part], axis=0)
    reduced = lax.psum_scatter(
        stacked.astype(jnp.bfloat16), "row", scatter_dimension=1, tiled=True
    ).astype(jnp.float32)
    reduced = lax.psum_scatter(reduced, "col", scatter_dimension=2, tiled=True)
    rows_own = reduced.shape[1]
    cols_own = reduced.shape[2]
    grad_zero = reduced[0]
    grad_ctrl = reduced[1:10].reshape(3, 3, rows_own, cols_own)
    grad_in = reduced[10:19].reshape(3, 3, rows_own, cols_own)
    return (grad_zero, grad_ctrl, grad_in)


def solution(mesh):
    in_specs = (
        P("row", "col", None),
        P("row", "col", None),
        P("row", "col", None),
        P("row", "col", None),
        P("row", "col", None),
        P(),
        P(),
        P(),
    )
    out_specs = (P("row", "col"), P(None, None, "row", "col"), P(None, None, "row", "col"))
    return jax.shard_map(
        on_device, mesh=mesh, in_specs=in_specs, out_specs=out_specs, check_vma=False
    )
```

profile of v0, /device:TPU:0, one launch (start us, length us, event | category | flops | bytes accessed | tf_op | source)
XLA Modules:
  0.0 227.2 jit_solution(15623551209118459208)
XLA Ops:
  8.1 2.4 %collective-permute-start = (bf16[1,32,320]{2,1,0:T(8,128)(2,1)S(1)}, bf16[1,32,320]{2,1,0:T(8,128)(2,1)S(1)}, u32[]{:S(2)}, u32[]{:S(2)}) collective-permute-start(bf16[1,32,320]{2,1,0:T(8,128)(2,1)S(1)} %get-tuple-element.57), channel_id=1, source_target_pairs={{0,4},{4,8},{8,12},{12,16},{16,20},{20,24},{24,28},{1,5},{5,9},{9,... | collective-permute-start | bytes 61448 | tf_op jit(solution)/shard_map/ppermute | solution.py:15
  11.8 3.8 %collective-permute-done.1 = bf16[1,32,320]{2,1,0:T(8,128)(2,1)S(1)} collective-permute-done((bf16[1,32,320]{2,1,0:T(8,128)(2,1)S(1)}, bf16[1,32,320]{2,1,0:T(8,128)(2,1)S(1)}, u32[]{:S(2)}, u32[]{:S(2)}) %collective-permute-start.1) | collective-permute-done | bytes 20512 | tf_op jit(solution)/shard_map/ppermute | solution.py:17
  15.6 2.0 pad_maximum_fusion.8
  19.0 4.5 %collective-permute-start.3 = (bf16[34,1,320]{2,1,0:T(2,128)(2,1)S(1)}, bf16[34,1,320]{2,1,0:T(2,128)(2,1)S(1)}, u32[]{:S(2)}, u32[]{:S(2)}) collective-permute-start(bf16[34,1,320]{2,1,0:T(2,128)(2,1)S(1)} %get-tuple-element.48), channel_id=1, source_target_pairs={{0,1},{1,2},{2,3},{4,5},{5,6},{6,7},{8,9},{9,10},{10,11},{12,13},{... | collective-permute-start | bytes 65288 | tf_op jit(solution)/shard_map/ppermute | solution.py:15
  25.4 3.0 %pad_maximum_fusion.7 = (bf16[32,32,320]{2,1,0:T(8,128)(2,1)S(1)}, bf16[32,32,320]{2,1,0:T(8,128)(2,1)S(1)}, bf16[32,32,320]{2,1,0:T(8,128)(2,1)S(1)}, bf16[32,3...) fusion(bf16[34,1,320]{2,1,0:T(2,128)(2,1)S(1)} %collective-permute-done.2, ...), kind=kLoop, calls=%fused_computation.140 | loop fusion | flops 7864320 | bytes 4672000 | tf_op jit(solution)/shard_map/concatenate | solution.py:13
  32.2 1.7 fusion.20
  33.9 1.9 copy.148
  37.4 3.3 %collective-permute-start.8 = (bf16[1,32,320]{1,2,0:T(8,128)(2,1)S(1)}, bf16[1,32,320]{1,2,0:T(8,128)(2,1)S(1)}, u32[]{:S(2)}, u32[]{:S(2)}) collective-permute-start(bf16[1,32,320]{1,2,0:T(8,128)(2,1)S(1)} %get-tuple-element.58), channel_id=1, source_target_pairs={{0,4},{4,8},{8,12},{12,16},{16,20},{20,24},{24,28},{1,5},{5,9},{9,... | collective-permute-start | bytes 61448 | tf_op jit(solution)/shard_map/ppermute | solution.py:15
  42.9 1.6 collective-permute-done.9
  46.4 5.1 %collective-permute-start.11 = (bf16[34,1,320]{2,1,0:T(2,128)(2,1)S(1)}, bf16[34,1,320]{2,1,0:T(2,128)(2,1)S(1)}, u32[]{:S(2)}, u32[]{:S(2)}) collective-permute-start(bf16[34,1,320]{2,1,0:T(2,128)(2,1)S(1)} %get-tuple-element.42), channel_id=1, source_target_pairs={{0,1},{1,2},{2,3},{4,5},{5,6},{6,7},{8,9},{9,10},{10,11},{12,13},{... | collective-permute-start | bytes 65288 | tf_op jit(solution)/shard_map/ppermute | solution.py:15
  58.6 1.7 copy.163
  60.3 2.4 %fusion.18 = (bf16[32,32,320]{2,1,0:T(8,128)(2,1)S(1)}, bf16[32,32,320]{2,1,0:T(8,128)(2,1)S(1)}) fusion(f32[32,32,320]{2,1,0:T(8,128)} %bitcast.306, bf16[32,32,320]{2,1,0:T(8,128)(2,1)} %param.11), kind=kLoop, calls=%fused_computation.27 | loop fusion | flops 3932160 | bytes 3276800 | tf_op jit(solution)/shard_map/convert_element_type | solution.py:93
  62.7 4.1 %collective-permute-start.4 = (bf16[1,32,640]{2,1,0:T(8,128)(2,1)S(1)}, bf16[1,32,640]{2,1,0:T(8,128)(2,1)S(1)}, u32[]{:S(2)}, u32[]{:S(2)}) collective-permute-start(bf16[1,32,640]{2,1,0:T(8,128)(2,1)S(1)} %get-tuple-element.24), channel_id=1, source_target_pairs={{0,4},{4,8},{8,12},{12,16},{16,20},{20,24},{24,28},{1,5},{5,9},{9,... | collective-permute-start | bytes 122888 | tf_op jit(solution)/shard_map/ppermute | solution.py:15
  70.5 4.3 %collective-permute-start.6 = (bf16[34,1,640]{2,1,0:T(2,128)(2,1)S(1)}, bf16[34,1,640]{2,1,0:T(2,128)(2,1)S(1)}, u32[]{:S(2)}, u32[]{:S(2)}) collective-permute-start(bf16[34,1,640]{2,1,0:T(2,128)(2,1)S(1)} %get-tuple-element.21), channel_id=1, source_target_pairs={{0,1},{1,2},{2,3},{4,5},{5,6},{6,7},{8,9},{9,10},{10,11},{12,13},{... | collective-permute-start | bytes 130568 | tf_op jit(solution)/shard_map/ppermute | solution.py:15
  76.9 4.3 %collective-permute-done.7 = bf16[34,1,640]{2,1,0:T(2,128)(2,1)S(1)} collective-permute-done((bf16[34,1,640]{2,1,0:T(2,128)(2,1)S(1)}, bf16[34,1,640]{2,1,0:T(2,128)(2,1)S(1)}, u32[]{:S(2)}, u32[]{:S(2)}) %collective-permute-start.7) | collective-permute-done | bytes 43552 | tf_op jit(solution)/shard_map/ppermute | solution.py:17
  81.2 3.2 %pad_maximum_fusion = (bf16[34,33,640]{2,1,0:T(8,128)(2,1)S(1)}, bf16[34,33,640]{2,1,0:T(8,128)(2,1)S(1)}) fusion(bf16[34,1,640]{2,1,0:T(2,128)(2,1)S(1)} %collective-permute-done.7, bf16[1,32,640]{2,1,0:T(8,128)(2,1)S(1)} %collective-permute-done.5, bf16[32,32,320]{2,1,0:T(8,128)(2,1)S(1)} %fusion.10, bf16[32,32,320]{2,1,0:T(8,128)(2,1)S(1)} %get-tuple-element.50, ...), kind=kLoop, calls=%fused_computation.8 | loop fusion | flops 14361600 | bytes 4352000 | tf_op jit(solution)/shard_map/concatenate | solution.py:13
  96.0 1.5 fusion.50
  103.4 1.5 fusion.40
  107.9 1.5 fusion.34
  109.4 8.9 %copy.173 = bf16[19,320,320]{2,0,1:T(8,128)(2,1)} copy(bf16[19,320,320]{1,2,0:T(8,128)(2,1)} %fusion.34) | data formatting | bytes 7782400 | tf_op jit(solution)/shard_map/concatenate | solution.py:96
  118.3 63.3 %reduce-scatter.5.cloned.1.call-done = bf16[19,40,320]{2,0,1:T(8,128)(2,1)} async-done(((bf16[19,320,320]{2,0,1:T(8,128)(2,1)}), bf16[19,40,320]{2,0,1:T(8,128)(2,1)}) %reduce-scatter.5.cloned.1.call-update) | async-done | bytes 486416 | tf_op jit(solution)/shard_map/reduce_scatter | solution.py:97
  182.8 3.4 %copy.202 = f32[19,40,320]{1,0,2:T(8,128)} copy(f32[19,40,320]{2,1,0:T(8,128)S(1)} %copy_convert_fusion) | data formatting | bytes 1945600
  186.2 3.9 %reshape.157 = f32[320,760]{1,0:T(8,128)} reshape(f32[320,19,40]{2,1,0:T(8,128)} %bitcast.301) | data formatting | bytes 1945600
  190.1 26.4 %reduce-scatter.7.cloned.1.call-done = f32[80,760]{1,0:T(8,128)} async-done(((f32[320,760]{1,0:T(8,128)}), f32[80,760]{1,0:T(8,128)}) %reduce-scatter.7.cloned.1.call-update) | async-done | bytes 243216
  (103 shorter events, 53.0 us)
Async XLA Ops:
  7.2 61.0 %copy-start = (bf16[32,32,320]{2,1,0:T(8,128)(2,1)S(1)}, bf16[32,32,320]{2,1,0:T(8,128)(2,1)}, u32[]{:S(2)}) copy-start(bf16[32,32,320]{2,1,0:T(8,128)(2,1)} %param.10) | copy-start | bytes 1966084
  7.2 174.4 %reduce-scatter.5.cloned.1.call-start = ((), (), s32[]{:S(2)}) async-start(), calls=%async_computation.2 | async-start | bytes 6635520 | tf_op jit(solution)/shard_map/reduce_scatter | solution.py:97
  8.1 3.7 %collective-permute-start = (bf16[1,32,320]{2,1,0:T(8,128)(2,1)S(1)}, bf16[1,32,320]{2,1,0:T(8,128)(2,1)S(1)}, u32[]{:S(2)}, u32[]{:S(2)}) collective-permute-start(bf16[1,32,320]{2,1,0:T(8,128)(2,1)S(1)} %get-tuple-element.57), channel_id=1, source_target_pairs={{0,4},{4,8},{8,12},{12,16},{16,20},{20,24},{24,28},{1,5},{5,9},{9,... | collective-permute-start | bytes 61448 | tf_op jit(solution)/shard_map/ppermute | solution.py:15
  10.4 5.2 %collective-permute-start.1 = (bf16[1,32,320]{2,1,0:T(8,128)(2,1)S(1)}, bf16[1,32,320]{2,1,0:T(8,128)(2,1)S(1)}, u32[]{:S(2)}, u32[]{:S(2)}) collective-permute-start(bf16[1,32,320]{2,1,0:T(8,128)(2,1)S(1)} %get-tuple-element.56), channel_id=1, source_target_pairs={{4,0},{8,4},{12,8},{16,12},{20,16},{24,20},{28,24},{5,1},{9,5},{13... | collective-permute-start | bytes 61448 | tf_op jit(solution)/shard_map/ppermute | solution.py:17
  11.8 11.8 %copy-start.6 = (bf16[3,3,320,320]{3,2,1,0:T(8,128)(2,1)S(1)}, bf16[3,3,320,320]{3,2,1,0:T(8,128)(2,1)}, u32[]{:S(2)}) copy-start(bf16[3,3,320,320]{3,2,1,0:T(8,128)(2,1)} %param.13) | copy-start | bytes 5529604
  17.7 6.9 %collective-permute-start.2 = (bf16[34,1,320]{2,1,0:T(2,128)(2,1)S(1)}, bf16[34,1,320]{2,1,0:T(2,128)(2,1)S(1)}, u32[]{:S(2)}, u32[]{:S(2)}) collective-permute-start(bf16[34,1,320]{2,1,0:T(2,128)(2,1)S(1)} %get-tuple-element.47), channel_id=1, source_target_pairs={{1,0},{2,1},{3,2},{5,4},{6,5},{7,6},{9,8},{10,9},{11,10},{13,12},{... | collective-permute-start | bytes 65288 | tf_op jit(solution)/shard_map/ppermute | solution.py:17
  19.0 6.3 %collective-permute-start.3 = (bf16[34,1,320]{2,1,0:T(2,128)(2,1)S(1)}, bf16[34,1,320]{2,1,0:T(2,128)(2,1)S(1)}, u32[]{:S(2)}, u32[]{:S(2)}) collective-permute-start(bf16[34,1,320]{2,1,0:T(2,128)(2,1)S(1)} %get-tuple-element.48), channel_id=1, source_target_pairs={{0,1},{1,2},{2,3},{4,5},{5,6},{6,7},{8,9},{9,10},{10,11},{12,13},{... | collective-permute-start | bytes 65288 | tf_op jit(solution)/shard_map/ppermute | solution.py:15
  30.0 1.1 copy-start.2
  33.9 1.9 copy-start.9
  36.4 5.6 %copy-start.3 = (bf16[32,32,320]{2,1,0:T(8,128)(2,1)}, bf16[32,32,320]{2,1,0:T(8,128)(2,1)S(1)}, u32[]{:S(2)}) copy-start(bf16[32,32,320]{2,1,0:T(8,128)(2,1)S(1)} %fusion.6) | copy-start | bytes 1966084
  36.4 5.6 %copy-start.7 = (bf16[32,32,320]{2,1,0:T(8,128)(2,1)S(1)}, bf16[32,32,320]{2,1,0:T(8,128)(2,1)}, u32[]{:S(2)}) copy-start(bf16[32,32,320]{2,1,0:T(8,128)(2,1)} %param.12) | copy-start | bytes 1966084
  37.4 5.5 %collective-permute-start.8 = (bf16[1,32,320]{1,2,0:T(8,128)(2,1)S(1)}, bf16[1,32,320]{1,2,0:T(8,128)(2,1)S(1)}, u32[]{:S(2)}, u32[]{:S(2)}) collective-permute-start(bf16[1,32,320]{1,2,0:T(8,128)(2,1)S(1)} %get-tuple-element.58), channel_id=1, source_target_pairs={{0,4},{4,8},{8,12},{12,16},{16,20},{20,24},{24,28},{1,5},{5,9},{9,... | collective-permute-start | bytes 61448 | tf_op jit(solution)/shard_map/ppermute | solution.py:15
  40.7 3.8 %collective-permute-start.9 = (bf16[1,32,320]{1,2,0:T(8,128)(2,1)S(1)}, bf16[1,32,320]{1,2,0:T(8,128)(2,1)S(1)}, u32[]{:S(2)}, u32[]{:S(2)}) collective-permute-start(bf16[1,32,320]{1,2,0:T(8,128)(2,1)S(1)} %get-tuple-element.59), channel_id=1, source_target_pairs={{4,0},{8,4},{12,8},{16,12},{20,16},{24,20},{28,24},{5,1},{9,5},{13... | collective-permute-start | bytes 61448 | tf_op jit(solution)/shard_map/ppermute | solution.py:17
  44.6 6.8 %copy-start.5 = (bf16[3,3,320,320]{3,2,1,0:T(8,128)(2,1)S(1)}, bf16[3,3,320,320]{3,2,1,0:T(8,128)(2,1)}, u32[]{:S(2)}) copy-start(bf16[3,3,320,320]{3,2,1,0:T(8,128)(2,1)} %param.15) | copy-start | bytes 5529604
  45.0 7.0 %collective-permute-start.10 = (bf16[34,1,320]{2,1,0:T(2,128)(2,1)S(1)}, bf16[34,1,320]{2,1,0:T(2,128)(2,1)S(1)}, u32[]{:S(2)}, u32[]{:S(2)}) collective-permute-start(bf16[34,1,320]{2,1,0:T(2,128)(2,1)S(1)} %get-tuple-element.43), channel_id=1, source_target_pairs={{1,0},{2,1},{3,2},{5,4},{6,5},{7,6},{9,8},{10,9},{11,10},{13,12},{... | collective-permute-start | bytes 65288 | tf_op jit(solution)/shard_map/ppermute | solution.py:17
  46.4 6.6 %collective-permute-start.11 = (bf16[34,1,320]{2,1,0:T(2,128)(2,1)S(1)}, bf16[34,1,320]{2,1,0:T(2,128)(2,1)S(1)}, u32[]{:S(2)}, u32[]{:S(2)}) collective-permute-start(bf16[34,1,320]{2,1,0:T(2,128)(2,1)S(1)} %get-tuple-element.42), channel_id=1, source_target_pairs={{0,1},{1,2},{2,3},{4,5},{5,6},{6,7},{8,9},{9,10},{10,11},{12,13},{... | collective-permute-start | bytes 65288 | tf_op jit(solution)/shard_map/ppermute | solution.py:15
  60.2 7.9 %copy-start.4 = (bf16[32,32,320]{2,1,0:T(8,128)(2,1)S(1)}, bf16[32,32,320]{2,1,0:T(8,128)(2,1)}, u32[]{:S(2)}) copy-start(bf16[32,32,320]{2,1,0:T(8,128)(2,1)} %copy-done.3) | copy-start | bytes 1966084
  62.7 6.7 %collective-permute-start.4 = (bf16[1,32,640]{2,1,0:T(8,128)(2,1)S(1)}, bf16[1,32,640]{2,1,0:T(8,128)(2,1)S(1)}, u32[]{:S(2)}, u32[]{:S(2)}) collective-permute-start(bf16[1,32,640]{2,1,0:T(8,128)(2,1)S(1)} %get-tuple-element.24), channel_id=1, source_target_pairs={{0,4},{4,8},{8,12},{12,16},{16,20},{20,24},{24,28},{1,5},{5,9},{9,... | collective-permute-start | bytes 122888 | tf_op jit(solution)/shard_map/ppermute | solution.py:15
  66.9 3.4 %collective-permute-start.5 = (bf16[1,32,640]{2,1,0:T(8,128)(2,1)S(1)}, bf16[1,32,640]{2,1,0:T(8,128)(2,1)S(1)}, u32[]{:S(2)}, u32[]{:S(2)}) collective-permute-start(bf16[1,32,640]{2,1,0:T(8,128)(2,1)S(1)} %get-tuple-element.25), channel_id=1, source_target_pairs={{4,0},{8,4},{12,8},{16,12},{20,16},{24,20},{28,24},{5,1},{9,5},{13... | collective-permute-start | bytes 122888 | tf_op jit(solution)/shard_map/ppermute | solution.py:17
  70.5 6.3 %collective-permute-start.6 = (bf16[34,1,640]{2,1,0:T(2,128)(2,1)S(1)}, bf16[34,1,640]{2,1,0:T(2,128)(2,1)S(1)}, u32[]{:S(2)}, u32[]{:S(2)}) collective-permute-start(bf16[34,1,640]{2,1,0:T(2,128)(2,1)S(1)} %get-tuple-element.21), channel_id=1, source_target_pairs={{0,1},{1,2},{2,3},{4,5},{5,6},{6,7},{8,9},{9,10},{10,11},{12,13},{... | collective-permute-start | bytes 130568 | tf_op jit(solution)/shard_map/ppermute | solution.py:15
  74.8 6.4 %collective-permute-start.7 = (bf16[34,1,640]{2,1,0:T(2,128)(2,1)S(1)}, bf16[34,1,640]{2,1,0:T(2,128)(2,1)S(1)}, u32[]{:S(2)}, u32[]{:S(2)}) collective-permute-start(bf16[34,1,640]{2,1,0:T(2,128)(2,1)S(1)} %get-tuple-element.20), channel_id=1, source_target_pairs={{1,0},{2,1},{3,2},{5,4},{6,5},{7,6},{9,8},{10,9},{11,10},{13,12},{... | collective-permute-start | bytes 130568 | tf_op jit(solution)/shard_map/ppermute | solution.py:17
  100.5 1.5 copy-start.8
  118.3 98.2 %reduce-scatter.7.cloned.1.call-start = ((), (), s32[]{:S(2)}) async-start(), calls=%async_computation.3 | async-start | bytes 1228800
  217.7 2.6 %copy-start.1 = (bf16[32,32,320]{2,1,0:T(8,128)(2,1)S(1)}, bf16[32,32,320]{2,1,0:T(8,128)(2,1)}, u32[]{:S(2)}) copy-start(bf16[32,32,320]{2,1,0:T(8,128)(2,1)} %param.10) | copy-start | bytes 1966084
  (1 other events, 0.9 us)
Sparse Core Ops, SparseCore 0:
  118.4 63.1 reduce-scatter.4
  190.2 26.2 reduce-scatter.6
where the time goes:
time: 228 us; the launch traced here: 227 us
  waiting for transfers between devices  102 us (45%)
  matrix products  36.8 us (16%)
  starting transfers between devices  31.7 us (14%)
  local copies, waits for them, and re-layouts  27.3 us (12%)
  other arithmetic  14.7 us (6%)
  between operations  14.6 us (6%)
    reduce_scatter x1, waiting for transfers between devices, on_device(): lax.psum_scatter(stacked.astype(jnp.bfloat16), 'row', scatter_dimension=1...  63.3 us
    unnamed x3, waiting for transfers between devices  26.4 us
    dot_general x18, matrix products, weight_local(): lax.dot_general(window, flat_grad, (((0,), (0,)), ((), ())), preferred_el...  24.3 us
    ppermute x6, starting transfers between devices, with_halo(): lax.ppermute(tail, axis, [(i, (i + 1) % count) for i in range(ends)])  23.7 us
    unnamed x29, local copies, waits for them, and re-layouts  11.9 us
    dot_general x18, matrix products, transpose_local(): lax.dot_general(window, kernel[tap_row, tap_col], (((1,), (1,)), ((), ())...  10.8 us
    ppermute x6, waiting for transfers between devices, with_halo(): lax.ppermute(head, axis, [((i + 1) % count, i) for i in range(ends)])  10.6 us
    concatenate x8, other arithmetic, with_halo(): jnp.concatenate([lax.ppermute(tail, axis, [(i, (i + 1) % count) for i in...  9.99 us
  transfers between devices with their start and end apart: 14, of which 8 were waited for; matrix products, arithmetic and copies ran while one was open for 2% of the time, Pallas kernels for 0%

commit v1 on v0

v1 whole, which is shorter than its diff:
```python
import functools

import jax
import jax.numpy as jnp
from jax import lax
from jax.experimental import pallas as pl
from jax.experimental.pallas import tpu as pltpu
from jax.sharding import PartitionSpec as P

BF16 = jnp.bfloat16
F32 = jnp.float32


def up(size, step):
    return -(-size // step) * step


def slope(values):
    sigm = jax.nn.sigmoid(values)
    return sigm * (1.0 + values * (1.0 - sigm))


def dot_nn(a, b):
    return lax.dot_general(a, b, (((1,), (0,)), ((), ())), preferred_element_type=F32)


def dot_nt(a, b):
    return lax.dot_general(a, b, (((1,), (1,)), ((), ())), preferred_element_type=F32)


class Plan:
    def __init__(self, height, width, channels, n_row, n_col):
        self.h, self.w, self.c = height, width, channels
        self.n_row, self.n_col = n_row, n_col
        self.cr, self.cc = channels // n_row, channels // n_col
        self.full = channels // 256 * 256
        self.rem = channels - self.full
        self.k1 = 3 * self.full + up(3 * self.rem, 256)
        wide = up(self.cc, 128)
        self.pq = wide if n_col * wide <= 2 * channels else self.cc
        self.np = n_col * self.pq
        self.qw = up(3 * self.cc, 128)
        self.rw = up(3 * self.cr, 128)
        self.hp = up(height + 2, 8)
        self.ring = 2 * width + 2 * self.hp
        self.px = height * width
        self.ls1 = 3 * self.qw + self.pq
        self.ls2 = 3 * self.rw


def spread(values, groups, size, pitch):
    rows = values.shape[0]
    pieces = []
    for g in range(groups):
        pieces.append(values[:, g * size : (g + 1) * size])
        if pitch > size:
            pieces.append(jnp.zeros((rows, pitch - size), values.dtype))
    return jnp.concatenate(pieces, axis=1)


def three_way(taps, starts, size, pitch):
    rows = taps[0].shape[0]
    pieces = []
    for s in starts:
        for t in taps:
            pieces.append(t[:, s : s + size])
        if pitch > 3 * size:
            pieces.append(jnp.zeros((rows, pitch - 3 * size), taps[0].dtype))
    return jnp.concatenate(pieces, axis=1)


def next_col(x, last):
    return jnp.concatenate([x[1:], last], axis=0)


def prev_col(x, first):
    return jnp.concatenate([first, x[:-1]], axis=0)


def prep_kernel(p, dw, cw, zw, mid, out, dec, w1, w2, zwp, out_t, act_t, slope_t, slope_dec):
    w1[...] = jnp.zeros_like(w1)
    zwp[...] = jnp.zeros_like(zwp)
    for a in range(3):
        for b in range(3):
            for q in range(p.n_col):
                rows = dw[3 * a + b, q * p.cc : (q + 1) * p.cc, :]
                at = q * p.pq
                base = a * p.k1
                w1[at : at + p.cc, base + b * p.full : base + (b + 1) * p.full] = rows[:, : p.full]
                if p.rem:
                    lane = base + 3 * p.full + b * p.rem
                    w1[at : at + p.cc, lane : lane + p.rem] = rows[:, p.full :]
    wide = p.n_col * p.qw
    for a in range(3):
        taps = [cw[3 * a + b] for b in range(3)]
        w2[:, a * wide : (a + 1) * wide] = three_way(
            taps, [q * p.cc for q in range(p.n_col)], p.cc, p.qw
        )
    for q in range(p.n_col):
        zwp[q * p.pq : q * p.pq + p.cc, :] = spread(
            zw[q * p.cc : (q + 1) * p.cc, :], p.n_col, p.cc, p.pq
        )
    step = 128

    def block(i, carry):
        at = pl.multiple_of(i * step, step)
        v = mid[pl.ds(at, step), :].astype(F32)
        s = jax.nn.sigmoid(v)
        act_t[:, pl.ds(at, step)] = (v * s).T.astype(BF16)
        slope_t[:, pl.ds(at, step)] = (s * (1.0 + v * (1.0 - s))).T
        out_t[:, pl.ds(at, step)] = out[pl.ds(at, step), :].astype(F32).T.astype(BF16)
        slope_dec[pl.ds(at, step), :] = spread(
            slope(dec[pl.ds(at, step), :].astype(F32)), p.n_col, p.cc, p.pq
        )
        return carry

    lax.fori_loop(0, p.px // step, block, 0)


def prep(p, dw, cw, zw, mid, out, dec):
    shape = jax.ShapeDtypeStruct
    return pl.pallas_call(
        functools.partial(prep_kernel, p),
        out_shape=(
            shape((p.np, 3 * p.k1), BF16),
            shape((p.c, 3 * p.n_col * p.qw), BF16),
            shape((p.np, p.np), BF16),
            shape((p.c, p.px), BF16),
            shape((p.c, p.px), BF16),
            shape((p.c, p.px), F32),
            shape((p.px, p.np), F32),
        ),
        cost_estimate=pl.CostEstimate(
            flops=2_000_000_000, bytes_accessed=20_000_000, transcendentals=3 * p.px * p.c
        ),
        name="prep",
    )(dw, cw, zw, mid, out, dec)


def act_kernel(p, x_ref, top, bottom, left, right, a_in, edge):
    edge[0, : p.h + 2, :] = left[3, : p.h + 2, :].astype(F32)
    edge[1, : p.h + 2, :] = right[3, : p.h + 2, :].astype(F32)

    def put(r, x):
        x = x.astype(F32)
        taps = (prev_col(x, edge[0, pl.ds(r, 1), :]), x, next_col(x, edge[1, pl.ds(r, 1), :]))
        taps = [(t * jax.nn.sigmoid(t)).astype(BF16) for t in taps]
        at = pl.multiple_of(r * p.w, p.w)
        a_in[pl.ds(at, p.w), :] = three_way(
            taps, [g * p.cr for g in range(p.n_row)], p.cr, p.rw
        )

    put(0, top[3])
    put(p.h + 1, bottom[3])

    def body(i, carry):
        put(i + 1, x_ref[i])
        return carry

    lax.fori_loop(0, p.h, body, 0)


def act_columns(p, ctrl_in, top, bottom, left, right):
    return pl.pallas_call(
        functools.partial(act_kernel, p),
        out_shape=jax.ShapeDtypeStruct(((p.h + 2) * p.w, p.n_row * p.rw), BF16),
        scratch_shapes=[pltpu.VMEM((2, up(p.h + 2, 8), p.c), F32)],
        cost_estimate=pl.CostEstimate(
            flops=1_000_000_000, bytes_accessed=4_000_000, transcendentals=3 * p.px * p.c
        ),
        name="act_columns",
    )(ctrl_in, top, bottom, left, right)


def store_slots(p, source, keep, send):
    mine = lax.axis_index("row")
    label = lax.axis_index("col")
    label = label ^ (label >> 1)
    for rr in range(p.n_row):
        r = rr ^ mine
        target = send if rr & 1 else keep
        for qq in range(p.n_col):
            q = qq ^ label
            shift = 1
            gray = q
            while (1 << shift) <= p.n_col:
                gray = gray ^ (q >> shift)
                shift += 1
            target[rr >> 1, qq] = source(r, gray).astype(BF16)


def first_kernel(
    p, go, top, bottom, left, right, own_l, own_r, w1, zwp, out_t, act_t, slope_dec,
    g2, keep, send, g1, ring_in, strips, dec, dec_ring, cg, cg_ring, grads,
):
    rows = p.h + 4
    strips[...] = jnp.zeros_like(strips)
    for k, s in enumerate((own_l[0], left[1], left[0], right[1], right[0], own_r[1])):
        strips[k, :rows, :] = s.astype(F32)

    def lanes(taps):
        pieces = [t[:, : p.full] for t in taps]
        if p.rem:
            pieces += [t[:, p.full :] for t in taps]
        pad = p.k1 - 3 * p.c
        if pad:
            pieces.append(jnp.zeros((taps[0].shape[0], pad), BF16))
        return jnp.concatenate(pieces, axis=1)

    def put(i, x):
        x = x.astype(F32)
        taps = (next_col(x, strips[4, pl.ds(i, 1), :]), x, prev_col(x, strips[1, pl.ds(i, 1), :]))
        at = pl.multiple_of(i * p.w, p.w)
        g1[pl.ds(at, p.w), :] = lanes([t.astype(BF16) for t in taps])

    for k in range(2):
        put(k, top[k])
        put(p.h + 2 + k, bottom[k])

    def body(i, carry):
        put(i + 2, go[i])
        return carry

    lax.fori_loop(0, p.h, body, 0)

    w, hp = p.w, p.hp
    for a in range(3):
        ls = slice(a * p.k1, (a + 1) * p.k1)
        ring_in[:w, ls] = g1[(2 - a) * w : (3 - a) * w, :]
        ring_in[w : 2 * w, ls] = g1[(p.h + 3 - a) * w : (p.h + 4 - a) * w, :]
        for side in range(2):
            taps = [strips[3 * side + b, 2 - a : 2 - a + hp, :].astype(BF16) for b in range(3)]
            ring_in[2 * w + side * hp : 2 * w + (side + 1) * hp, ls] = lanes(taps)

    weights = w1[...]
    step = 256
    for m in range(p.px // step):
        at = m * step
        lhs = jnp.concatenate(
            [g1[(3 - a) * w + at : (3 - a) * w + at + step, :] for a in range(3)], axis=1
        )
        dec[at : at + step, :] = (
            dot_nt(lhs, weights) * slope_dec[at : at + step, :]
        ).astype(BF16)

    row, col = lax.axis_index("row"), lax.axis_index("col")
    has_top = (row > 0).astype(F32)
    has_bottom = (row < p.n_row - 1).astype(F32)
    has_left = (col > 0).astype(F32)
    has_right = (col < p.n_col - 1).astype(F32)
    line = lax.broadcasted_iota(jnp.int32, (hp, p.np), 0)
    corner = jnp.where(line == 0, has_top, jnp.where(line == p.h + 1, has_bottom, 1.0))
    sections = (
        (top[2], 0, w, has_top),
        (bottom[2], w, w, has_bottom),
        (left[2], 2 * w, hp, corner * has_left),
        (right[2], 2 * w + hp, hp, corner * has_right),
    )
    ring_back = dot_nt(ring_in[...], weights)
    for pre, at, size, mask in sections:
        pre = pre.astype(F32)
        if pre.shape[0] < size:
            pre = jnp.concatenate([pre, jnp.zeros((size - pre.shape[0], p.c), F32)], axis=0)
        factor = spread(slope(pre[:size]), p.n_col, p.cc, p.pq) * mask
        dec_ring[at : at + size, :] = (ring_back[at : at + size] * factor).astype(BF16)

    zero = dot_nn(out_t[...], dec[...])
    for q in range(p.n_col):
        for r in range(p.n_row):
            grads[q, r, : p.cr, 3 * p.qw :] = zero[
                r * p.cr : (r + 1) * p.cr, q * p.pq : (q + 1) * p.pq
            ]
    for m in range(p.px // step):
        cg[m * step : (m + 1) * step, :] = dot_nt(dec[m * step : (m + 1) * step, :], zwp[...])
    cg_ring[...] = dot_nt(dec_ring[...], zwp[...])

    def put2(r, x):
        taps = (
            next_col(x, cg_ring[pl.ds(2 * w + hp + r, 1), :]),
            x,
            prev_col(x, cg_ring[pl.ds(2 * w + r, 1), :]),
        )
        at = pl.multiple_of(r * w, w)
        g2[pl.ds(at, w), :] = three_way(
            [t.astype(BF16) for t in taps], [q * p.pq for q in range(p.n_col)], p.cc, p.qw
        )

    put2(0, cg_ring[:w, :])
    put2(p.h + 1, cg_ring[w : 2 * w, :])

    def body2(i, carry):
        put2(i + 1, cg[pl.ds(pl.multiple_of(i * w, w), w), :])
        return carry

    lax.fori_loop(0, p.h, body2, 0)

    for a in range(3):
        for q in range(p.n_col):
            tap = dot_nn(
                act_t[...], g2[(2 - a) * w : (2 - a) * w + p.px, q * p.qw : (q + 1) * p.qw]
            )
            for r in range(p.n_row):
                grads[q, r, : p.cr, a * p.qw : (a + 1) * p.qw] = tap[r * p.cr : (r + 1) * p.cr]
    store_slots(p, lambda r, q: grads[q, r, : p.cr, :], keep, send)


def first(p, go, top, bottom, left, right, own_l, own_r, w1, zwp, out_t, act_t, slope_dec):
    shape = jax.ShapeDtypeStruct
    slots = shape((p.n_row // 2, p.n_col, p.cr, p.ls1), BF16)
    return pl.pallas_call(
        functools.partial(first_kernel, p),
        out_shape=(shape(((p.h + 2) * p.w, p.n_col * p.qw), BF16), slots, slots),
        scratch_shapes=[
            pltpu.VMEM(((p.h + 4) * p.w, p.k1), BF16),
            pltpu.VMEM((p.ring, 3 * p.k1), BF16),
            pltpu.VMEM((6, up(p.hp + 2, 8), p.c), F32),
            pltpu.VMEM((p.px, p.np), BF16),
            pltpu.VMEM((p.ring, p.np), BF16),
            pltpu.VMEM((p.px, p.np), F32),
            pltpu.VMEM((p.ring, p.np), F32),
            pltpu.VMEM((p.n_col, p.n_row, up(p.cr, 8), p.ls1), F32),
        ],
        cost_estimate=pl.CostEstimate(
            flops=10_000_000_000, bytes_accessed=20_000_000, transcendentals=0
        ),
        name="first",
    )(go, top, bottom, left, right, own_l, own_r, w1, zwp, out_t, act_t, slope_dec)


def second_kernel(p, g2, a_in, w2, slope_t, keep, send, mid, grads):
    w = p.w
    step = 256
    for m in range(p.px // step):
        at = m * step
        rhs = jnp.concatenate(
            [g2[(2 - a) * w + at : (2 - a) * w + at + step, :] for a in range(3)], axis=1
        )
        mid[:, at : at + step] = (
            dot_nt(w2[...], rhs) * slope_t[:, at : at + step]
        ).astype(BF16)
    for a in range(3):
        for r in range(p.n_row):
            tap = dot_nn(mid[...], a_in[a * w : a * w + p.px, r * p.rw : (r + 1) * p.rw])
            for q in range(p.n_col):
                grads[r, q, : p.cc, a * p.rw : (a + 1) * p.rw] = tap[q * p.cc : (q + 1) * p.cc]
    store_slots(p, lambda r, q: grads[r, q, : p.cc, :], keep, send)


def second(p, g2, a_in, w2, slope_t):
    slots = jax.ShapeDtypeStruct((p.n_row // 2, p.n_col, p.cc, p.ls2), BF16)
    return pl.pallas_call(
        functools.partial(second_kernel, p),
        out_shape=(slots, slots),
        scratch_shapes=[
            pltpu.VMEM((p.c, p.px), BF16),
            pltpu.VMEM((p.n_row, p.n_col, up(p.cc, 8), p.ls2), F32),
        ],
        cost_estimate=pl.CostEstimate(
            flops=6_000_000_000, bytes_accessed=10_000_000, transcendentals=0
        ),
        name="second",
    )(g2, a_in, w2, slope_t)


def gray(i):
    return i ^ (i >> 1)


def swap(values, axis, bit):
    count = lax.axis_size(axis)
    if axis == "row":
        pairs = [(i, i ^ (1 << bit)) for i in range(count)]
    else:
        place = {gray(i): i for i in range(count)}
        pairs = [(i, place[gray(i) ^ (1 << bit)]) for i in range(count)]
    return lax.ppermute(values, axis, pairs)


def total(pieces):
    summed = pieces[0].astype(F32)
    for piece in pieces[1:]:
        summed = summed + piece.astype(F32)
    return summed


class Chain:
    def __init__(self, pieces, order):
        self.pieces, self.order = pieces, list(order)
        self.dims = sorted(order)

    def step(self):
        dim = self.order.pop(0)
        at = self.dims.index(dim)
        self.dims.pop(at)
        rank = self.pieces[0].ndim
        other = tuple([slice(None)] * at + [1])
        own = tuple([slice(None)] * at + [0])
        sent = total([x[other] for x in self.pieces]).astype(BF16)
        axis, bit = dim[1], dim[2]
        self.pieces = [x[own] for x in self.pieces] + [swap(sent, axis, bit)]


def dims_of(p):
    k_row = p.n_row.bit_length() - 1
    k_col = p.n_col.bit_length() - 1
    row = [(i, "row", k_row - 1 - i) for i in range(k_row - 1)]
    col = [(len(row) + i, "col", k_col - 1 - i) for i in range(k_col)]
    return row, col


def as_cube(p, values):
    row, col = dims_of(p)
    return values.reshape((2,) * (len(row) + len(col)) + values.shape[2:])


def last_kernel(p, n1, *refs):
    gz, gc, gi = refs[-3:]
    one = jnp.concatenate([x[...] for x in refs[:n1]], axis=1)
    gz[...] = one[:, 3 * p.qw : 3 * p.qw + p.cc]
    for a in range(3):
        for b in range(3):
            at = a * p.qw + b * p.cc
            gc[a, b] = one[:, at : at + p.cc]
    two = jnp.concatenate([x[...] for x in refs[n1:-3]], axis=0).T
    for a in range(3):
        for b in range(3):
            at = a * p.rw + b * p.cr
            gi[a, b] = two[at : at + p.cr, :]


def last(p, chains1, chains2):
    shape = jax.ShapeDtypeStruct
    return pl.pallas_call(
        functools.partial(last_kernel, p, len(chains1)),
        out_shape=(
            shape((p.cr, p.cc), F32),
            shape((3, 3, p.cr, p.cc), F32),
            shape((3, 3, p.cr, p.cc), F32),
        ),
        name="last",
    )(*[total(c.pieces) for c in chains1 + chains2])


def halos(p, go, dec_pre, ctrl_in):
    count = lax.axis_size("row")
    down = [(i, i + 1) for i in range(count - 1)]
    upward = [(i + 1, i) for i in range(count - 1)]
    top = lax.ppermute(
        jnp.concatenate([go[-2:], dec_pre[-1:], ctrl_in[-1:]], axis=0), "row", down
    )
    bottom = lax.ppermute(
        jnp.concatenate([go[:2], dec_pre[:1], ctrl_in[:1]], axis=0), "row", upward
    )
    grad = jnp.concatenate([top[:2], go, bottom[:2]], axis=0)
    spare = jnp.zeros((2, 1, p.c), BF16)

    def strip(g0, g1, edge):
        return jnp.stack(
            [
                grad[:, g0],
                grad[:, g1],
                jnp.concatenate([top[2:3, edge], dec_pre[:, edge], bottom[2:3, edge], spare[:, 0]]),
                jnp.concatenate([top[3:4, edge], ctrl_in[:, edge], bottom[3:4, edge], spare[:, 0]]),
            ]
        )

    own_l = strip(0, 1, 0)
    own_r = strip(p.w - 2, p.w - 1, p.w - 1)
    count = lax.axis_size("col")
    forward = [(i, i + 1) for i in range(count - 1)]
    backward = [(i + 1, i) for i in range(count - 1)]
    left = lax.ppermute(own_r, "col", forward)
    right = lax.ppermute(own_l, "col", backward)
    return top, bottom, left, right, own_l, own_r


def on_device(grad_out, dec_pre, ctrl_out, ctrl_mid, ctrl_in, dec_weight, zero_weight, ctrl_weight):
    height, width, channels = grad_out.shape
    p = Plan(height, width, channels, lax.axis_size("row"), lax.axis_size("col"))
    flat = (p.px, p.c)
    taps = (9, p.c, p.c)
    w1, w2, zwp, out_t, act_t, slope_t, slope_dec = prep(
        p,
        dec_weight.reshape(taps),
        ctrl_weight.reshape(taps),
        zero_weight,
        ctrl_mid.reshape(flat),
        ctrl_out.reshape(flat),
        dec_pre.reshape(flat),
    )
    top, bottom, left, right, own_l, own_r = halos(p, grad_out, dec_pre, ctrl_in)
    g2, keep1, send1 = first(
        p, grad_out, top, bottom, left, right, own_l, own_r, w1, zwp, out_t, act_t, slope_dec
    )
    row, col = dims_of(p)
    got1 = swap(send1, "row", 0)
    a_in = act_columns(p, ctrl_in, top, bottom, left, right)
    keep2, send2 = second(p, g2, a_in, w2, slope_t)
    chains1 = [Chain([as_cube(p, keep1), as_cube(p, got1)], row[::-1] + col)]
    chains1[0].step()
    got2 = swap(send2, "row", 0)
    cubes = [as_cube(p, keep2), as_cube(p, got2)]
    half = p.cc // 2 if (p.cc // 2) % 8 == 0 else p.cc
    parts = [(0, half), (half, p.cc)] if half < p.cc else [(0, p.cc)]
    orders = [col + row, col[::-1] + row[::-1]]
    chains2 = [
        Chain([x[..., lo:hi, :] for x in cubes], order) for (lo, hi), order in zip(parts, orders)
    ]
    live = chains1 + chains2
    while any(c.order for c in live):
        for c in live:
            if c.order:
                c.step()
    return last(p, chains1, chains2)


def solution(mesh):
    in_specs = (
        P("row", "col", None),
        P("row", "col", None),
        P("row", "col", None),
        P("row", "col", None),
        P("row", "col", None),
        P(),
        P(),
        P(),
    )
    out_specs = (P("row", "col"), P(None, None, "row", "col"), P(None, None, "row", "col"))
    return jax.shard_map(
        on_device, mesh=mesh, in_specs=in_specs, out_specs=out_specs, check_vma=False
    )
```

time: 228 us -> 119 us (0.52)
  waiting for transfers between devices: 102 us -> 20.9 us
  Pallas kernels: 0 us -> 49.5 us
  matrix products: 36.8 us -> 0 us
  local copies, waits for them, and re-layouts: 27.3 us -> 9.49 us
  between operations: 14.6 us -> 0.96 us
  other arithmetic: 14.7 us -> 3.31 us
  starting transfers between devices: 31.7 us -> 34.5 us
    reduce_scatter x1 -> x0, waiting for transfers between devices: 63.3 us -> none  [on_device(): lax.psum_scatter(stacked.astype(jnp.bfloat16), 'row', scatter_dimension=1...]
    pallas_call x0 -> x5, Pallas kernels: none -> 49.5 us  [the longest x1 19 us: first(): pl.pallas_call(functools.partial(first_kernel, p), out_shape=(shape(((p.h...]
    dot_general x38 -> x0, matrix products: 36.8 us -> none  [the longest x18 24.3 us: weight_local(): lax.dot_general(window, flat_grad, (((0,), (0,)), ((), ())), preferred_el...]
    unnamed x3 -> x0, waiting for transfers between devices: 26.4 us -> none
    concatenate x8 -> x2, other arithmetic: 9.99 us -> 0.37 us  [the longest x1 0.19 us: halos(): jnp.concatenate([go[-2:], dec_pre[-1:], ctrl_in[-1:]], axis=0)]
    unnamed x29 -> x21, local copies, waits for them, and re-layouts: 11.9 us -> 2.91 us
    concatenate x2 -> x1, local copies, waits for them, and re-layouts: 8.88 us -> 0.08 us  [strip(): jnp.concatenate([top[2:3, edge], dec_pre[:, edge], bottom[2:3, edge], spa...]
    ppermute x12 -> x18, waiting for transfers between devices: 12.3 us -> 20.9 us  [the longest x14 19.3 us: swap(): return lax.ppermute(values, axis, pairs)]
  transfers between devices with their start and end apart: 14 -> 18, of which waited for: 8 -> 9; matrix products, arithmetic and copies ran while one was open for 2% -> 6% of each run, Pallas kernels for 0% -> 9%
where the time goes in v1:
time: 119 us
  Pallas kernels  49.5 us (42%)
  starting transfers between devices  34.5 us (29%)
  waiting for transfers between devices  20.9 us (18%)
  local copies, waits for them, and re-layouts  9.49 us (8%)
  other arithmetic  3.31 us (3%)
    ppermute x14, starting transfers between devices, swap(): return lax.ppermute(values, axis, pairs)  25 us
    ppermute x14, waiting for transfers between devices, swap(): return lax.ppermute(values, axis, pairs)  19.3 us
    pallas_call x1, Pallas kernels, first(): pl.pallas_call(functools.partial(first_kernel, p), out_shape=(shape(((p.h...  19 us
    pallas_call x1, Pallas kernels, second(): pl.pallas_call(functools.partial(second_kernel, p), out_shape=(slots, slo...  11.1 us
    pallas_call x1, Pallas kernels, prep(): pl.pallas_call(functools.partial(prep_kernel, p), out_shape=(shape((p.np,...  10.4 us
    pallas_call x1, Pallas kernels, act_columns(): pl.pallas_call(functools.partial(act_kernel, p), out_shape=jax.ShapeDtype...  7.22 us
    ppermute x1, starting transfers between devices, halos(): left = lax.ppermute(own_r, 'col', forward)  4.55 us
    unnamed x21, local copies, waits for them, and re-layouts  2.91 us
  transfers between devices with their start and end apart: 18, of which 9 were waited for; matrix products, arithmetic and copies ran while one was open for 6% of the time, Pallas kernels for 9%

profile of v1, /device:TPU:0, one launch (start us, length us, event | category | flops | bytes accessed | tf_op | source)
XLA Modules:
  0.0 118.7 jit_solution(15990318130760453582)
XLA Ops:
  0.6 1.4 %copy.33 = bf16[32,32,320]{2,0,1:T(8,128)(2,1)S(1)} copy(bf16[32,32,320]{2,1,0:T(8,128)(2,1)} %go.1) | data formatting | bytes 1310720 | tf_op args[0]
  3.9 2.4 %collective-permute-start = (bf16[4,32,320]{2,0,1:T(4,128)(2,1)S(1)}, bf16[4,32,320]{2,0,1:T(4,128)(2,1)S(1)}, u32[]{:S(2)}, u32[]{:S(2)}) collective-permute-start(bf16[4,32,320]{2,0,1:T(4,128)(2,1)S(1)} %pad_maximum_fusion.2), channel_id=1, source_target_pairs={{0,4},{4,8},{8,12},{12,16},{16,20},{20,24},{24,28},{1,5},{5,9},{9,... | collective-permute-start | bytes 245768 | tf_op jit(solution)/shard_map/ppermute | solution.py:448
  10.3 1.6 %collective-permute-done.1 = bf16[4,32,320]{2,0,1:T(4,128)(2,1)S(1)} collective-permute-done((bf16[4,32,320]{2,0,1:T(4,128)(2,1)S(1)}, bf16[4,32,320]{2,0,1:T(4,128)(2,1)S(1)}, u32[]{:S(2)}, u32[]{:S(2)}) %collective-permute-start.1) | collective-permute-done | bytes 81952 | tf_op jit(solution)/shard_map/ppermute | solution.py:451
  13.5 4.6 %collective-permute-start.2 = (bf16[4,36,320]{2,1,0:T(8,128)(2,1)S(1)}, bf16[4,36,320]{2,1,0:T(8,128)(2,1)S(1)}, u32[]{:S(2)}, u32[]{:S(2)}) collective-permute-start(bf16[4,36,320]{2,1,0:T(8,128)(2,1)S(1)} %pad_maximum_fusion.own_r), channel_id=1, source_target_pairs={{0,1},{1,2},{2,3},{4,5},{5,6},{6,7},{8,9},{9,10},{10,11},{12,13},{... | collective-permute-start | bytes 276488 | tf_op jit(solution)/shard_map/ppermute | solution.py:472
  18.1 10.4 %prep.1 = (bf16[512,3072]{1,0:T(8,128)(2,1)}, bf16[320,3072]{1,0:T(8,128)(2,1)}, bf16[512,512]{1,0:T(8,128)(2,1)}, bf16[320,1024]{1,0:T(8,128)(2,1)}, bf16[320,1...) custom-call(bf16[9,320,320]{2,1,0:T(8,128)(2,1)} %bitcast.208, bf16[9,320,320]{2,1,0:T(8,128)(2,1)} %bitcast.209, ...), custom_call_target="tpu_custom_call" | custom-call | flops 2000000000 | bytes 20000000 | tf_op jit(solution)/shard_map/prep/pallas_call | solution.py:122
  31.1 7.2 %act_columns.1.a_in = bf16[1088,1024]{1,0:T(8,128)(2,1)} custom-call(bf16[32,32,320]{2,1,0:T(8,128)(2,1)} %x_ref.1, bf16[4,32,320]{2,1,0:T(8,128)(2,1)} %copy.44.top, bf16[4,32,320]{2,1,0:T(8,128)(2,1)} %copy.45.bottom, bf16[4,36,320]{2,1,0:T(8,128)(2,1)} %copy-done.6, bf16[4,36,320]{2,1,0:T(8,128)(2,1)} %copy-done.5), custom_call_target="tpu_custom_call" | custom-call | flops 1000000000 | bytes 4000000 | tf_op jit(solution)/shard_map/act_columns/pallas_call | solution.py:164
  38.4 19.0 %first.1 = (bf16[1088,1024]{1,0:T(8,128)(2,1)}, bf16[4,4,40,896]{3,2,1,0:T(8,128)(2,1)}, bf16[4,4,40,896]{3,2,1,0:T(8,128)(2,1)}) custom-call(bf16[32,32,320]{2,1,0:T(8,128)(2,1)} %go.1, bf16[4,32,320]{2,1,0:T(8,128)(2,1)} %copy.44.top, bf16[4,32,320]{2,1,0:T(8,128)(2,1)} %copy.45.bottom, bf16[4,36,320]{2,1,0:T(8,128)(2,1)} %copy-done.6, ...), custom_call_target="tpu_custom_call" | custom-call | flops 10000000000 | bytes 20000000 | tf_op jit(solution)/shard_map/first/pallas_call | solution.py:310
  57.3 11.1 %second.1 = (bf16[4,4,80,384]{3,2,1,0:T(8,128)(2,1)}, bf16[4,4,80,384]{3,2,1,0:T(8,128)(2,1)}) custom-call(bf16[1088,1024]{1,0:T(8,128)(2,1)} %get-tuple-element.22.g2, bf16[1088,1024]{1,0:T(8,128)(2,1)} %act_columns.1.a_in, bf16[320,3072]{1,0:T(8,128)(2,1)} %get-tuple-element.23.w2, f32[320,1024]{1,0:T(8,128)} %get-tuple-element.24.slope_t), custom_call_target="tpu_custom_call" | custom-call | flops 6000000000 | bytes 10000000 | tf_op jit(solution)/shard_map/second/pallas_call | solution.py:351
  68.4 2.7 %collective-permute-start.9 = (bf16[4,4,80,384]{3,2,1,0:T(8,128)(2,1)}, bf16[4,4,80,384]{3,2,1,0:T(8,128)(2,1)S(1)}, u32[]{:S(2)}, u32[]{:S(2)}) collective-permute-start(bf16[4,4,80,384]{3,2,1,0:T(8,128)(2,1)} %get-tuple-element.26), channel_id=1, source_target_pairs={{0,4},{4,0},{8,12},{12,8},{16,20},{20,16},{24,28},{28,24},{1,5},{5... | collective-permute-start | bytes 2949128 | tf_op jit(solution)/shard_map/ppermute | solution.py:376
  73.6 1.6 %collective-permute-start.14 = (bf16[2,2,2,40,384]{4,3,1,0,2:T(8,128)(2,1)S(1)}, bf16[2,2,2,40,384]{4,3,1,0,2:T(8,128)(2,1)S(1)}, u32[]{:S(2)}, u32[]{:S(2)}) collective-permute-start(bf16[2,2,2,40,384]{4,3,1,0,2:T(8,128)(2,1)S(1)} %fusion.4), channel_id=1, source_target_pairs={{0,1},{1,0},{2,3},{3,2},{4,5},{5,4},{6,7},{7,6},{8,9},{9,8},{10,11... | collective-permute-start | bytes 737288 | tf_op jit(solution)/shard_map/ppermute | solution.py:376
  75.3 2.5 %collective-permute-start.10 = (bf16[2,2,2,40,384]{4,3,2,1,0:T(8,128)(2,1)S(1)}, bf16[2,2,2,40,384]{4,3,2,1,0:T(8,128)(2,1)S(1)}, u32[]{:S(2)}, u32[]{:S(2)}) collective-permute-start(bf16[2,2,2,40,384]{4,3,2,1,0:T(8,128)(2,1)S(1)} %fusion.3), channel_id=1, source_target_pairs={{0,3},{1,2},{2,1},{3,0},{4,7},{5,6},{6,5},{7,4},{8,11},{9,10},{10,... | collective-permute-start | bytes 737288 | tf_op jit(solution)/shard_map/ppermute | solution.py:376
  78.1 2.5 %collective-permute-start.5 = (bf16[2,2,2,40,896]{4,3,2,1,0:T(8,128)(2,1)S(1)}, bf16[2,2,2,40,896]{4,3,2,1,0:T(8,128)(2,1)S(1)}, u32[]{:S(2)}, u32[]{:S(2)}) collective-permute-start(bf16[2,2,2,40,896]{4,3,2,1,0:T(8,128)(2,1)S(1)} %fusion), channel_id=1, source_target_pairs={{0,8},{4,12},{8,0},{12,4},{16,24},{20,28},{24,16},{28,20},{1,9},{5... | collective-permute-start | bytes 1720328 | tf_op jit(solution)/shard_map/ppermute | solution.py:376
  82.0 2.4 %collective-permute-start.15 = (bf16[2,2,40,384]{3,2,1,0:T(8,128)(2,1)S(1)}, bf16[2,2,40,384]{3,2,1,0:T(8,128)(2,1)S(1)}, u32[]{:S(2)}, u32[]{:S(2)}) collective-permute-start(bf16[2,2,40,384]{3,2,1,0:T(8,128)(2,1)S(1)} %fusion.8), channel_id=1, source_target_pairs={{0,3},{1,2},{2,1},{3,0},{4,7},{5,6},{6,5},{7,4},{8,11},{9,10},{10,... | collective-permute-start | bytes 368648 | tf_op jit(solution)/shard_map/ppermute | solution.py:376
  84.3 5.6 %collective-permute-done.10 = bf16[2,2,2,40,384]{4,3,2,1,0:T(8,128)(2,1)S(1)} collective-permute-done((bf16[2,2,2,40,384]{4,3,2,1,0:T(8,128)(2,1)S(1)}, bf16[2,2,2,40,384]{4,3,2,1,0:T(8,128)(2,1)S(1)}, u32[]{:S(2)}, u32[]{:S(2)}) %collective-permute-start.10) | collective-permute-done | bytes 245792 | tf_op jit(solution)/shard_map/ppermute | solution.py:376
  90.8 1.6 %collective-permute-done.15 = bf16[2,2,40,384]{3,2,1,0:T(8,128)(2,1)S(1)} collective-permute-done((bf16[2,2,40,384]{3,2,1,0:T(8,128)(2,1)S(1)}, bf16[2,2,40,384]{3,2,1,0:T(8,128)(2,1)S(1)}, u32[]{:S(2)}, u32[]{:S(2)}) %collective-permute-start.15) | collective-permute-done | bytes 122912 | tf_op jit(solution)/shard_map/ppermute | solution.py:376
  92.5 2.5 %collective-permute-start.16 = (bf16[2,40,384]{2,1,0:T(8,128)(2,1)S(1)}, bf16[2,40,384]{2,1,0:T(8,128)(2,1)S(1)}, u32[]{:S(2)}, u32[]{:S(2)}) collective-permute-start(bf16[2,40,384]{2,1,0:T(8,128)(2,1)S(1)} %fusion.10), channel_id=1, source_target_pairs={{0,8},{4,12},{8,0},{12,4},{16,24},{20,28},{24,16},{28,20},{1,9},{5... | collective-permute-start | bytes 184328 | tf_op jit(solution)/shard_map/ppermute | solution.py:376
  95.0 1.9 %collective-permute-start.12 = (bf16[2,40,384]{2,1,0:T(8,128)(2,1)S(1)}, bf16[2,40,384]{2,1,0:T(8,128)(2,1)S(1)}, u32[]{:S(2)}, u32[]{:S(2)}) collective-permute-start(bf16[2,40,384]{2,1,0:T(8,128)(2,1)S(1)} %fusion.9), channel_id=1, source_target_pairs={{0,16},{4,20},{8,24},{12,28},{16,0},{20,4},{24,8},{28,12},{1,17},{... | collective-permute-start | bytes 184328 | tf_op jit(solution)/shard_map/ppermute | solution.py:376
  97.3 1.9 %collective-permute-start.17 = (bf16[40,384]{1,0:T(8,128)(2,1)S(1)}, bf16[40,384]{1,0:T(8,128)(2,1)S(1)}, u32[]{:S(2)}, u32[]{:S(2)}) collective-permute-start(bf16[40,384]{1,0:T(8,128)(2,1)S(1)} %fusion.11), channel_id=1, source_target_pairs={{0,16},{4,20},{8,24},{12,28},{16,0},{20,4},{24,8},{28,12},{1,17},{... | collective-permute-start | bytes 92168 | tf_op jit(solution)/shard_map/ppermute | solution.py:376
  100.0 2.4 %collective-permute-start.13 = (bf16[40,384]{1,0:T(8,128)(2,1)S(1)}, bf16[40,384]{1,0:T(8,128)(2,1)S(1)}, u32[]{:S(2)}, u32[]{:S(2)}) collective-permute-start(bf16[40,384]{1,0:T(8,128)(2,1)S(1)} %fusion.13), channel_id=1, source_target_pairs={{0,8},{4,12},{8,0},{12,4},{16,24},{20,28},{24,16},{28,20},{1,9},{5... | collective-permute-start | bytes 92168 | tf_op jit(solution)/shard_map/ppermute | solution.py:376
  102.3 2.1 %collective-permute-done.6 = bf16[2,2,40,896]{3,2,1,0:T(8,128)(2,1)S(1)} collective-permute-done((bf16[2,2,40,896]{3,2,1,0:T(8,128)(2,1)S(1)}, bf16[2,2,40,896]{3,2,1,0:T(8,128)(2,1)S(1)}, u32[]{:S(2)}, u32[]{:S(2)}) %collective-permute-start.6) | collective-permute-done | bytes 286752 | tf_op jit(solution)/shard_map/ppermute | solution.py:376
  106.6 5.1 %collective-permute-done.7 = bf16[2,40,896]{2,1,0:T(8,128)(2,1)S(1)} collective-permute-done((bf16[2,40,896]{2,1,0:T(8,128)(2,1)S(1)}, bf16[2,40,896]{2,1,0:T(8,128)(2,1)S(1)}, u32[]{:S(2)}, u32[]{:S(2)}) %collective-permute-start.7) | collective-permute-done | bytes 143392 | tf_op jit(solution)/shard_map/ppermute | solution.py:376
  111.7 2.0 %collective-permute-start.8 = (bf16[40,896]{1,0:T(8,128)(2,1)S(1)}, bf16[40,896]{1,0:T(8,128)(2,1)S(1)}, u32[]{:S(2)}, u32[]{:S(2)}) collective-permute-start(bf16[40,896]{1,0:T(8,128)(2,1)S(1)} %fusion.5), channel_id=1, source_target_pairs={{0,1},{1,0},{2,3},{3,2},{4,5},{5,4},{6,7},{7,6},{8,9},{9,8},{10,11... | collective-permute-start | bytes 215048 | tf_op jit(solution)/shard_map/ppermute | solution.py:376
  114.4 1.7 %collective-permute-done.8 = bf16[40,896]{1,0:T(8,128)(2,1)S(1)} collective-permute-done((bf16[40,896]{1,0:T(8,128)(2,1)S(1)}, bf16[40,896]{1,0:T(8,128)(2,1)S(1)}, u32[]{:S(2)}, u32[]{:S(2)}) %collective-permute-start.8) | collective-permute-done | bytes 71712 | tf_op jit(solution)/shard_map/ppermute | solution.py:376
  116.8 1.8 %last.1 = (f32[40,80]{1,0:T(8,128)}, f32[3,3,40,80]{3,2,1,0:T(8,128)}, f32[3,3,40,80]{3,2,1,0:T(8,128)}) custom-call(f32[40,896]{1,0:T(8,128)} %fusion.6.refs_0_, f32[40,384]{1,0:T(8,128)} %fusion.14.refs_1_, f32[40,384]{1,0:T(8,128)} %fusion.12.refs_2_), custom_call_target="tpu_custom_call" | custom-call | tf_op jit(solution)/shard_map/last/pallas_call | solution.py:433
  (81 shorter events, 19.9 us)
Async XLA Ops:
  3.9 6.3 %collective-permute-start = (bf16[4,32,320]{2,0,1:T(4,128)(2,1)S(1)}, bf16[4,32,320]{2,0,1:T(4,128)(2,1)S(1)}, u32[]{:S(2)}, u32[]{:S(2)}) collective-permute-start(bf16[4,32,320]{2,0,1:T(4,128)(2,1)S(1)} %pad_maximum_fusion.2), channel_id=1, source_target_pairs={{0,4},{4,8},{8,12},{12,16},{16,20},{20,24},{24,28},{1,5},{5,9},{9,... | collective-permute-start | bytes 245768 | tf_op jit(solution)/shard_map/ppermute | solution.py:448
  6.6 5.3 %collective-permute-start.1 = (bf16[4,32,320]{2,0,1:T(4,128)(2,1)S(1)}, bf16[4,32,320]{2,0,1:T(4,128)(2,1)S(1)}, u32[]{:S(2)}, u32[]{:S(2)}) collective-permute-start(bf16[4,32,320]{2,0,1:T(4,128)(2,1)S(1)} %pad_maximum_fusion.3), channel_id=1, source_target_pairs={{4,0},{8,4},{12,8},{16,12},{20,16},{24,20},{28,24},{5,1},{9,5},{13... | collective-permute-start | bytes 245768 | tf_op jit(solution)/shard_map/ppermute | solution.py:451
  12.2 16.4 %copy-start.2 = (bf16[4,36,320]{2,1,0:T(8,128)(2,1)}, bf16[4,36,320]{2,1,0:T(8,128)(2,1)S(1)}, u32[]{:S(2)}) copy-start(bf16[4,36,320]{2,1,0:T(8,128)(2,1)S(1)} %pad_maximum_fusion.1.own_l) | copy-start | bytes 276484
  12.2 17.7 %collective-permute-start.3 = (bf16[4,36,320]{2,1,0:T(8,128)(2,1)S(1)}, bf16[4,36,320]{2,1,0:T(8,128)(2,1)S(1)}, u32[]{:S(2)}, u32[]{:S(2)}) collective-permute-start(bf16[4,36,320]{2,1,0:T(8,128)(2,1)S(1)} %pad_maximum_fusion.1.own_l), channel_id=1, source_target_pairs={{1,0},{2,1},{3,2},{5,4},{6,5},{7,6},{9,8},{10,9},{11,10},{13,12},{... | collective-permute-start | bytes 276488 | tf_op jit(solution)/shard_map/ppermute | solution.py:473
  13.5 15.0 %copy-start.3 = (bf16[4,36,320]{2,1,0:T(8,128)(2,1)}, bf16[4,36,320]{2,1,0:T(8,128)(2,1)S(1)}, u32[]{:S(2)}) copy-start(bf16[4,36,320]{2,1,0:T(8,128)(2,1)S(1)} %pad_maximum_fusion.own_r) | copy-start | bytes 276484
  13.5 16.3 %collective-permute-start.2 = (bf16[4,36,320]{2,1,0:T(8,128)(2,1)S(1)}, bf16[4,36,320]{2,1,0:T(8,128)(2,1)S(1)}, u32[]{:S(2)}, u32[]{:S(2)}) collective-permute-start(bf16[4,36,320]{2,1,0:T(8,128)(2,1)S(1)} %pad_maximum_fusion.own_r), channel_id=1, source_target_pairs={{0,1},{1,2},{2,3},{4,5},{5,6},{6,7},{8,9},{9,10},{10,11},{12,13},{... | collective-permute-start | bytes 276488 | tf_op jit(solution)/shard_map/ppermute | solution.py:472
  29.9 0.6 copy-start.5
  57.3 14.9 %copy-start.4 = (bf16[4,4,40,896]{3,2,1,0:T(8,128)(2,1)S(1)}, bf16[4,4,40,896]{3,2,1,0:T(8,128)(2,1)}, u32[]{:S(2)}) copy-start(bf16[4,4,40,896]{3,2,1,0:T(8,128)(2,1)} %get-tuple-element.21) | copy-start | bytes 3440644
  68.4 4.0 %copy-start.1 = (bf16[4,4,80,384]{3,2,1,0:T(8,128)(2,1)S(1)}, bf16[4,4,80,384]{3,2,1,0:T(8,128)(2,1)}, u32[]{:S(2)}) copy-start(bf16[4,4,80,384]{3,2,1,0:T(8,128)(2,1)} %get-tuple-element.25) | copy-start | bytes 2949124
  68.4 5.1 %collective-permute-start.9 = (bf16[4,4,80,384]{3,2,1,0:T(8,128)(2,1)}, bf16[4,4,80,384]{3,2,1,0:T(8,128)(2,1)S(1)}, u32[]{:S(2)}, u32[]{:S(2)}) collective-permute-start(bf16[4,4,80,384]{3,2,1,0:T(8,128)(2,1)} %get-tuple-element.26), channel_id=1, source_target_pairs={{0,4},{4,0},{8,12},{12,8},{16,20},{20,16},{24,28},{28,24},{1,5},{5... | collective-permute-start | bytes 2949128 | tf_op jit(solution)/shard_map/ppermute | solution.py:376
  72.2 5.7 %collective-permute-start.4 = (bf16[4,4,40,896]{3,2,1,0:T(8,128)(2,1)S(1)}, bf16[4,4,40,896]{3,2,1,0:T(8,128)(2,1)S(1)}, u32[]{:S(2)}, u32[]{:S(2)}) collective-permute-start(bf16[4,4,40,896]{3,2,1,0:T(8,128)(2,1)S(1)} %copy-done.4), channel_id=1, source_target_pairs={{0,4},{4,0},{8,12},{12,8},{16,20},{20,16},{24,28},{28,24},{1,5},{5... | collective-permute-start | bytes 3440648 | tf_op jit(solution)/shard_map/ppermute | solution.py:376
  73.6 4.3 %copy-start = (bf16[4,4,40,896]{3,2,1,0:T(8,128)(2,1)S(1)}, bf16[4,4,40,896]{3,2,1,0:T(8,128)(2,1)}, u32[]{:S(2)}) copy-start(bf16[4,4,40,896]{3,2,1,0:T(8,128)(2,1)} %get-tuple-element.20) | copy-start | bytes 3440644
  73.6 8.3 %collective-permute-start.14 = (bf16[2,2,2,40,384]{4,3,1,0,2:T(8,128)(2,1)S(1)}, bf16[2,2,2,40,384]{4,3,1,0,2:T(8,128)(2,1)S(1)}, u32[]{:S(2)}, u32[]{:S(2)}) collective-permute-start(bf16[2,2,2,40,384]{4,3,1,0,2:T(8,128)(2,1)S(1)} %fusion.4), channel_id=1, source_target_pairs={{0,1},{1,0},{2,3},{3,2},{4,5},{5,4},{6,7},{7,6},{8,9},{9,8},{10,11... | collective-permute-start | bytes 737288 | tf_op jit(solution)/shard_map/ppermute | solution.py:376
  75.3 14.5 %collective-permute-start.10 = (bf16[2,2,2,40,384]{4,3,2,1,0:T(8,128)(2,1)S(1)}, bf16[2,2,2,40,384]{4,3,2,1,0:T(8,128)(2,1)S(1)}, u32[]{:S(2)}, u32[]{:S(2)}) collective-permute-start(bf16[2,2,2,40,384]{4,3,2,1,0:T(8,128)(2,1)S(1)} %fusion.3), channel_id=1, source_target_pairs={{0,3},{1,2},{2,1},{3,0},{4,7},{5,6},{6,5},{7,4},{8,11},{9,10},{10,... | collective-permute-start | bytes 737288 | tf_op jit(solution)/shard_map/ppermute | solution.py:376
  78.1 18.8 %collective-permute-start.5 = (bf16[2,2,2,40,896]{4,3,2,1,0:T(8,128)(2,1)S(1)}, bf16[2,2,2,40,896]{4,3,2,1,0:T(8,128)(2,1)S(1)}, u32[]{:S(2)}, u32[]{:S(2)}) collective-permute-start(bf16[2,2,2,40,896]{4,3,2,1,0:T(8,128)(2,1)S(1)} %fusion), channel_id=1, source_target_pairs={{0,8},{4,12},{8,0},{12,4},{16,24},{20,28},{24,16},{28,20},{1,9},{5... | collective-permute-start | bytes 1720328 | tf_op jit(solution)/shard_map/ppermute | solution.py:376
  82.0 10.5 %collective-permute-start.15 = (bf16[2,2,40,384]{3,2,1,0:T(8,128)(2,1)S(1)}, bf16[2,2,40,384]{3,2,1,0:T(8,128)(2,1)S(1)}, u32[]{:S(2)}, u32[]{:S(2)}) collective-permute-start(bf16[2,2,40,384]{3,2,1,0:T(8,128)(2,1)S(1)} %fusion.8), channel_id=1, source_target_pairs={{0,3},{1,2},{2,1},{3,0},{4,7},{5,6},{6,5},{7,4},{8,11},{9,10},{10,... | collective-permute-start | bytes 368648 | tf_op jit(solution)/shard_map/ppermute | solution.py:376
  89.9 5.0 %collective-permute-start.11 = (bf16[2,2,40,384]{3,2,1,0:T(8,128)(2,1)S(1)}, bf16[2,2,40,384]{3,2,1,0:T(8,128)(2,1)S(1)}, u32[]{:S(2)}, u32[]{:S(2)}) collective-permute-start(bf16[2,2,40,384]{3,2,1,0:T(8,128)(2,1)S(1)} %fusion.7), channel_id=1, source_target_pairs={{0,1},{1,0},{2,3},{3,2},{4,5},{5,4},{6,7},{7,6},{8,9},{9,8},{10,11... | collective-permute-start | bytes 368648 | tf_op jit(solution)/shard_map/ppermute | solution.py:376
  92.5 4.8 %collective-permute-start.16 = (bf16[2,40,384]{2,1,0:T(8,128)(2,1)S(1)}, bf16[2,40,384]{2,1,0:T(8,128)(2,1)S(1)}, u32[]{:S(2)}, u32[]{:S(2)}) collective-permute-start(bf16[2,40,384]{2,1,0:T(8,128)(2,1)S(1)} %fusion.10), channel_id=1, source_target_pairs={{0,8},{4,12},{8,0},{12,4},{16,24},{20,28},{24,16},{28,20},{1,9},{5... | collective-permute-start | bytes 184328 | tf_op jit(solution)/shard_map/ppermute | solution.py:376
  95.0 4.9 %collective-permute-start.12 = (bf16[2,40,384]{2,1,0:T(8,128)(2,1)S(1)}, bf16[2,40,384]{2,1,0:T(8,128)(2,1)S(1)}, u32[]{:S(2)}, u32[]{:S(2)}) collective-permute-start(bf16[2,40,384]{2,1,0:T(8,128)(2,1)S(1)} %fusion.9), channel_id=1, source_target_pairs={{0,16},{4,20},{8,24},{12,28},{16,0},{20,4},{24,8},{28,12},{1,17},{... | collective-permute-start | bytes 184328 | tf_op jit(solution)/shard_map/ppermute | solution.py:376
  97.0 7.5 %collective-permute-start.6 = (bf16[2,2,40,896]{3,2,1,0:T(8,128)(2,1)S(1)}, bf16[2,2,40,896]{3,2,1,0:T(8,128)(2,1)S(1)}, u32[]{:S(2)}, u32[]{:S(2)}) collective-permute-start(bf16[2,2,40,896]{3,2,1,0:T(8,128)(2,1)S(1)} %fusion.1), channel_id=1, source_target_pairs={{0,16},{4,20},{8,24},{12,28},{16,0},{20,4},{24,8},{28,12},{1,17},{... | collective-permute-start | bytes 860168 | tf_op jit(solution)/shard_map/ppermute | solution.py:376
  97.3 8.6 %collective-permute-start.17 = (bf16[40,384]{1,0:T(8,128)(2,1)S(1)}, bf16[40,384]{1,0:T(8,128)(2,1)S(1)}, u32[]{:S(2)}, u32[]{:S(2)}) collective-permute-start(bf16[40,384]{1,0:T(8,128)(2,1)S(1)} %fusion.11), channel_id=1, source_target_pairs={{0,16},{4,20},{8,24},{12,28},{16,0},{20,4},{24,8},{28,12},{1,17},{... | collective-permute-start | bytes 92168 | tf_op jit(solution)/shard_map/ppermute | solution.py:376
  100.0 13.8 %collective-permute-start.13 = (bf16[40,384]{1,0:T(8,128)(2,1)S(1)}, bf16[40,384]{1,0:T(8,128)(2,1)S(1)}, u32[]{:S(2)}, u32[]{:S(2)}) collective-permute-start(bf16[40,384]{1,0:T(8,128)(2,1)S(1)} %fusion.13), channel_id=1, source_target_pairs={{0,8},{4,12},{8,0},{12,4},{16,24},{20,28},{24,16},{28,20},{1,9},{5... | collective-permute-start | bytes 92168 | tf_op jit(solution)/shard_map/ppermute | solution.py:376
  104.5 7.2 %collective-permute-start.7 = (bf16[2,40,896]{2,1,0:T(8,128)(2,1)S(1)}, bf16[2,40,896]{2,1,0:T(8,128)(2,1)S(1)}, u32[]{:S(2)}, u32[]{:S(2)}) collective-permute-start(bf16[2,40,896]{2,1,0:T(8,128)(2,1)S(1)} %fusion.2), channel_id=1, source_target_pairs={{0,3},{1,2},{2,1},{3,0},{4,7},{5,6},{6,5},{7,4},{8,11},{9,10},{10,... | collective-permute-start | bytes 430088 | tf_op jit(solution)/shard_map/ppermute | solution.py:376
  111.7 4.4 %collective-permute-start.8 = (bf16[40,896]{1,0:T(8,128)(2,1)S(1)}, bf16[40,896]{1,0:T(8,128)(2,1)S(1)}, u32[]{:S(2)}, u32[]{:S(2)}) collective-permute-start(bf16[40,896]{1,0:T(8,128)(2,1)S(1)} %fusion.5), channel_id=1, source_target_pairs={{0,1},{1,0},{2,3},{3,2},{4,5},{5,4},{6,7},{7,6},{8,9},{9,8},{10,11... | collective-permute-start | bytes 215048 | tf_op jit(solution)/shard_map/ppermute | solution.py:376
  (1 other events, 0.6 us)

commit v2 on v1

--- a/solution.py
+++ b/solution.py
@@ -13,6 +13,14 @@
 
 def up(size, step):
     return -(-size // step) * step
+
+
+def vm(shape, dtype):
+    return pltpu.VMEM(shape, dtype)
+
+
+def near(*arrays):
+    return [pltpu.with_memory_space_constraint(x, pltpu.VMEM) for x in arrays]
 
 
 def slope(values):
@@ -114,25 +122,25 @@
         )
         return carry
 
-    lax.fori_loop(0, p.px // step, block, 0)
+    lax.fori_loop(0, p.px // step, block, 0, unroll=2)
 
 
 def prep(p, dw, cw, zw, mid, out, dec):
-    shape = jax.ShapeDtypeStruct
     return pl.pallas_call(
         functools.partial(prep_kernel, p),
         out_shape=(
-            shape((p.np, 3 * p.k1), BF16),
-            shape((p.c, 3 * p.n_col * p.qw), BF16),
-            shape((p.np, p.np), BF16),
-            shape((p.c, p.px), BF16),
-            shape((p.c, p.px), BF16),
-            shape((p.c, p.px), F32),
-            shape((p.px, p.np), F32),
+            vm((p.np, 3 * p.k1), BF16),
+            vm((p.c, 3 * p.n_col * p.qw), BF16),
+            vm((p.np, p.np), BF16),
+            vm((p.c, p.px), BF16),
+            vm((p.c, p.px), BF16),
+            vm((p.c, p.px), F32),
+            vm((p.px, p.np), F32),
         ),
         cost_estimate=pl.CostEstimate(
             flops=2_000_000_000, bytes_accessed=20_000_000, transcendentals=3 * p.px * p.c
         ),
+        compiler_params=pltpu.CompilerParams(vmem_limit_bytes=20 << 20),
         name="prep",
     )(dw, cw, zw, mid, out, dec)
 
@@ -157,17 +165,18 @@
         put(i + 1, x_ref[i])
         return carry
 
-    lax.fori_loop(0, p.h, body, 0)
+    lax.fori_loop(0, p.h, body, 0, unroll=8)
 
 
 def act_columns(p, ctrl_in, top, bottom, left, right):
     return pl.pallas_call(
         functools.partial(act_kernel, p),
-        out_shape=jax.ShapeDtypeStruct(((p.h + 2) * p.w, p.n_row * p.rw), BF16),
+        out_shape=vm(((p.h + 2) * p.w, p.n_row * p.rw), BF16),
         scratch_shapes=[pltpu.VMEM((2, up(p.h + 2, 8), p.c), F32)],
         cost_estimate=pl.CostEstimate(
             flops=1_000_000_000, bytes_accessed=4_000_000, transcendentals=3 * p.px * p.c
         ),
+        compiler_params=pltpu.CompilerParams(vmem_limit_bytes=8 << 20),
         name="act_columns",
     )(ctrl_in, top, bottom, left, right)
 
@@ -186,7 +195,7 @@
             while (1 << shift) <= p.n_col:
                 gray = gray ^ (q >> shift)
                 shift += 1
-            target[rr >> 1, qq] = source(r, gray).astype(BF16)
+            target[(rr >> 1) * p.n_col + qq] = source(r, gray).astype(BF16)
 
 
 def first_kernel(
@@ -221,7 +230,7 @@
         put(i + 2, go[i])
         return carry
 
-    lax.fori_loop(0, p.h, body, 0)
+    lax.fori_loop(0, p.h, body, 0, unroll=8)
 
     w, hp = p.w, p.hp
     for a in range(3):
@@ -292,7 +301,7 @@
         put2(i + 1, cg[pl.ds(pl.multiple_of(i * w, w), w), :])
         return carry
 
-    lax.fori_loop(0, p.h, body2, 0)
+    lax.fori_loop(0, p.h, body2, 0, unroll=8)
 
     for a in range(3):
         for q in range(p.n_col):
@@ -306,10 +315,10 @@
 
 def first(p, go, top, bottom, left, right, own_l, own_r, w1, zwp, out_t, act_t, slope_dec):
     shape = jax.ShapeDtypeStruct
-    slots = shape((p.n_row // 2, p.n_col, p.cr, p.ls1), BF16)
+    slots = vm((p.n_row // 2 * p.n_col, p.cr, p.ls1), BF16)
     return pl.pallas_call(
         functools.partial(first_kernel, p),
-        out_shape=(shape(((p.h + 2) * p.w, p.n_col * p.qw), BF16), slots, slots),
+        out_shape=(vm(((p.h + 2) * p.w, p.n_col * p.qw), BF16), slots, slots),
         scratch_shapes=[
             pltpu.VMEM(((p.h + 4) * p.w, p.k1), BF16),
             pltpu.VMEM((p.ring, 3 * p.k1), BF16),
@@ -323,8 +332,12 @@
         cost_estimate=pl.CostEstimate(
             flops=10_000_000_000, bytes_accessed=20_000_000, transcendentals=0
         ),
+        compiler_params=pltpu.CompilerParams(vmem_limit_bytes=28 << 20),
         name="first",
-    )(go, top, bottom, left, right, own_l, own_r, w1, zwp, out_t, act_t, slope_dec)
+    )(
+        go, top, bottom, left, right, own_l, own_r,
+        *near(w1, zwp, out_t, act_t, slope_dec),
+    )
 
 
 def second_kernel(p, g2, a_in, w2, slope_t, keep, send, mid, grads):
@@ -347,7 +360,7 @@
 
 
 def second(p, g2, a_in, w2, slope_t):
-    slots = jax.ShapeDtypeStruct((p.n_row // 2, p.n_col, p.cc, p.ls2), BF16)
+    slots = vm((p.n_row // 2 * p.n_col, p.cc, p.ls2), BF16)
     return pl.pallas_call(
         functools.partial(second_kernel, p),
         out_shape=(slots, slots),
@@ -358,87 +371,177 @@
         cost_estimate=pl.CostEstimate(
             flops=6_000_000_000, bytes_accessed=10_000_000, transcendentals=0
         ),
+        compiler_params=pltpu.CompilerParams(vmem_limit_bytes=16 << 20),
         name="second",
-    )(g2, a_in, w2, slope_t)
+    )(*near(g2, a_in, w2, slope_t))
 
 
 def gray(i):
     return i ^ (i >> 1)
 
 
-def swap(values, axis, bit):
+def swap(name, values, dim):
+    axis, bit = dim
     count = lax.axis_size(axis)
     if axis == "row":
         pairs = [(i, i ^ (1 << bit)) for i in range(count)]
     else:
         place = {gray(i): i for i in range(count)}
         pairs = [(i, place[gray(i) ^ (1 << bit)]) for i in range(count)]
-    return lax.ppermute(values, axis, pairs)
-
-
-def total(pieces):
-    summed = pieces[0].astype(F32)
-    for piece in pieces[1:]:
-        summed = summed + piece.astype(F32)
-    return summed
+    with jax.named_scope(name):
+        return lax.ppermute(values, axis, pairs)
+
+
+class Part:
+    def __init__(self, dims, rows, lanes, keep, got=None):
+        self.dims, self.rows, self.lanes = dims, rows, lanes
+        self.keep, self.got = keep, got
+
+
+def slot_of(bits, dims):
+    at = 0
+    for dim in dims:
+        at = 2 * at + bits[dim]
+    return at
+
+
+def assignments(dims):
+    for code in range(1 << len(dims)):
+        yield {dim: (code >> i) & 1 for i, dim in enumerate(dims)}
+
+
+def overlap(a, b):
+    lo, hi = max(a[0], b[0]), min(a[1], b[1])
+    return (lo, hi) if lo < hi else None
+
+
+def mix_kernel(sources, targets, *refs):
+    ins = refs[: 2 * len(sources)]
+    outs = refs[2 * len(sources) :]
+    for k, source in enumerate(sources):
+        keep, got = ins[2 * k], ins[2 * k + 1]
+        for n, target in enumerate(targets):
+            rows = overlap(source.rows, target.rows)
+            lanes = overlap(source.lanes, target.lanes)
+            if rows is None or lanes is None:
+                continue
+            sr = slice(rows[0] - source.rows[0], rows[1] - source.rows[0])
+            sl = slice(lanes[0] - source.lanes[0], lanes[1] - source.lanes[0])
+            tr = slice(rows[0] - target.rows[0], rows[1] - target.rows[0])
+            tl = slice(lanes[0] - target.lanes[0], lanes[1] - target.lanes[0])
+            for bits in assignments(source.dims):
+                at = slot_of(bits, source.dims)
+                value = keep[at, sr, sl].astype(F32) + got[at, sr, sl].astype(F32)
+                goes = bits[target.dims[0]]
+                out = outs[2 * n + goes]
+                out[slot_of(bits, target.dims[1:]), tr, tl] = value.astype(out.dtype)
+
+
+def mix(name, sources, targets):
+    shapes = []
+    for t in targets:
+        shape = (1 << (len(t.dims) - 1), t.rows[1] - t.rows[0], t.lanes[1] - t.lanes[0])
+        shapes += [vm(shape, F32), vm(shape, BF16)]
+    size = sum(s.keep.size for s in sources)
+    bare = [Part(s.dims, s.rows, s.lanes, None) for s in sources]
+    with jax.named_scope(name):
+        results = pl.pallas_call(
+            functools.partial(mix_kernel, bare, targets),
+            out_shape=tuple(shapes),
+            compiler_params=pltpu.CompilerParams(vmem_limit_bytes=6 << 20),
+            cost_estimate=pl.CostEstimate(
+                flops=200_000_000, bytes_accessed=8 * size, transcendentals=0
+            ),
+            name=name,
+        )(*near(*[x for s in sources for x in (s.keep, s.got)]))
+    return [
+        (Part(t.dims[1:], t.rows, t.lanes, results[2 * i]), results[2 * i + 1], t.dims[0])
+        for i, t in enumerate(targets)
+    ]
 
 
 class Chain:
-    def __init__(self, pieces, order):
-        self.pieces, self.order = pieces, list(order)
-        self.dims = sorted(order)
-
-    def step(self):
-        dim = self.order.pop(0)
-        at = self.dims.index(dim)
-        self.dims.pop(at)
-        rank = self.pieces[0].ndim
-        other = tuple([slice(None)] * at + [1])
-        own = tuple([slice(None)] * at + [0])
-        sent = total([x[other] for x in self.pieces]).astype(BF16)
-        axis, bit = dim[1], dim[2]
-        self.pieces = [x[own] for x in self.pieces] + [swap(sent, axis, bit)]
+    def __init__(self, name, rows, lanes, cut, dims, early, late):
+        self.name, self.rows, self.lanes, self.cut = name, rows, lanes, cut
+        self.early, self.late = early, late
+        self.whole = Part(dims, (0, rows), (0, lanes), None)
+        self.parts = []
+
+    def halves(self, order_a, order_b):
+        if self.cut[0] == "rows":
+            at = self.cut[1]
+            return [
+                Part(order_a, (0, at), (0, self.lanes), None),
+                Part(order_b, (at, self.rows), (0, self.lanes), None),
+            ]
+        at = self.cut[1]
+        return [
+            Part(order_a, (0, self.rows), (0, at), None),
+            Part(order_b, (0, self.rows), (at, self.lanes), None),
+        ]
+
+    def send(self, stage, mixed):
+        self.parts = []
+        for i, (part, sent, dim) in enumerate(mixed):
+            part.got = swap(f"{self.name}{stage}{'ab'[i]}", sent, dim)
+            self.parts.append(part)
+
+    def begin(self, keep, got):
+        self.whole.keep, self.whole.got = keep, got
+        e, l = self.early, self.late
+        self.send(1, mix(f"{self.name}mix1", [self.whole], self.halves(e + l, e[::-1] + l)))
+
+    def second(self):
+        mixed = []
+        for i, part in enumerate(self.parts):
+            target = Part(part.dims, part.rows, part.lanes, None)
+            mixed += mix(f"{self.name}mix2{'ab'[i]}", [part], [target])
+        self.send(2, mixed)
+
+    def third(self):
+        target = Part(self.late, (0, self.rows), (0, self.lanes), None)
+        self.send(3, mix(f"{self.name}mix3", self.parts, [target]))
+
+    def later(self, stage):
+        part = self.parts[0]
+        target = Part(part.dims, part.rows, part.lanes, None)
+        self.send(stage, mix(f"{self.name}mix{stage}", [part], [target]))
 
 
 def dims_of(p):
     k_row = p.n_row.bit_length() - 1
     k_col = p.n_col.bit_length() - 1
-    row = [(i, "row", k_row - 1 - i) for i in range(k_row - 1)]
-    col = [(len(row) + i, "col", k_col - 1 - i) for i in range(k_col)]
+    row = [("row", i) for i in range(k_row - 1, 0, -1)]
+    col = [("col", i) for i in range(k_col - 1, -1, -1)]
     return row, col
 
 
-def as_cube(p, values):
-    row, col = dims_of(p)
-    return values.reshape((2,) * (len(row) + len(col)) + values.shape[2:])
-
-
-def last_kernel(p, n1, *refs):
-    gz, gc, gi = refs[-3:]
-    one = jnp.concatenate([x[...] for x in refs[:n1]], axis=1)
+def last_kernel(p, keep1, got1, keep2, got2, gz, gc, gi):
+    one = keep1[0] + got1[0].astype(F32)
     gz[...] = one[:, 3 * p.qw : 3 * p.qw + p.cc]
     for a in range(3):
         for b in range(3):
             at = a * p.qw + b * p.cc
             gc[a, b] = one[:, at : at + p.cc]
-    two = jnp.concatenate([x[...] for x in refs[n1:-3]], axis=0).T
+    two = (keep2[0] + got2[0].astype(F32)).T
     for a in range(3):
         for b in range(3):
             at = a * p.rw + b * p.cr
             gi[a, b] = two[at : at + p.cr, :]
 
 
-def last(p, chains1, chains2):
+def last(p, one, two):
     shape = jax.ShapeDtypeStruct
     return pl.pallas_call(
-        functools.partial(last_kernel, p, len(chains1)),
+        functools.partial(last_kernel, p),
         out_shape=(
             shape((p.cr, p.cc), F32),
             shape((3, 3, p.cr, p.cc), F32),
             shape((3, 3, p.cr, p.cc), F32),
         ),
+        compiler_params=pltpu.CompilerParams(vmem_limit_bytes=8 << 20),
         name="last",
-    )(*[total(c.pieces) for c in chains1 + chains2])
+    )(*near(one.keep, one.got, two.keep, two.got))
 
 
 def halos(p, go, dec_pre, ctrl_in):
@@ -493,25 +596,24 @@
         p, grad_out, top, bottom, left, right, own_l, own_r, w1, zwp, out_t, act_t, slope_dec
     )
     row, col = dims_of(p)
-    got1 = swap(send1, "row", 0)
+    core = ("row", 0)
+    got1 = swap("onecore", send1, core)
     a_in = act_columns(p, ctrl_in, top, bottom, left, right)
+    one = Chain("one", p.cr, p.ls1, ("lanes", up(p.ls1 // 2, 128)), row + col, row, col)
+    one.begin(keep1, got1)
     keep2, send2 = second(p, g2, a_in, w2, slope_t)
-    chains1 = [Chain([as_cube(p, keep1), as_cube(p, got1)], row[::-1] + col)]
-    chains1[0].step()
-    got2 = swap(send2, "row", 0)
-    cubes = [as_cube(p, keep2), as_cube(p, got2)]
-    half = p.cc // 2 if (p.cc // 2) % 8 == 0 else p.cc
-    parts = [(0, half), (half, p.cc)] if half < p.cc else [(0, p.cc)]
-    orders = [col + row, col[::-1] + row[::-1]]
-    chains2 = [
-        Chain([x[..., lo:hi, :] for x in cubes], order) for (lo, hi), order in zip(parts, orders)
-    ]
-    live = chains1 + chains2
-    while any(c.order for c in live):
-        for c in live:
-            if c.order:
-                c.step()
-    return last(p, chains1, chains2)
+    got2 = swap("twocore", send2, core)
+    half = p.cc // 2
+    cut = ("rows", half) if half % 8 == 0 else ("lanes", up(p.ls2 // 2, 128))
+    two = Chain("two", p.cc, p.ls2, cut, row + col, col, row)
+    two.begin(keep2, got2)
+    for chain in (one, two):
+        for stage in range(2, len(chain.early) + 1):
+            chain.second()
+        chain.third()
+        for stage in range(4, len(chain.late) + 3):
+            chain.later(stage)
+    return last(p, one.parts[0], two.parts[0])
 
 
 def solution(mesh):

time: 119 us -> 81.8 us (0.69)
  Pallas kernels: 49.5 us -> 23.4 us
  waiting for transfers between devices: 20.9 us -> 15.9 us
  local copies, waits for them, and re-layouts: 9.49 us -> 6.49 us
  other arithmetic: 3.31 us -> 0.59 us
    pallas_call x4 -> x14, Pallas kernels: 38.4 us -> 16.9 us  [the longest x1 9.3 us: first(): pl.pallas_call(functools.partial(first_kernel, p), out_shape=(vm(((p.h +...]
    ppermute x14, waiting for transfers between devices: 19.3 us -> 12.3 us  [swap(): return lax.ppermute(values, axis, pairs)]
    pallas_call x1, Pallas kernels: 11.1 us -> 6.51 us  [second(): pl.pallas_call(functools.partial(second_kernel, p), out_shape=(slots, slo...]
    add x4 -> x0, other arithmetic: 2.04 us -> none  [total(): summed = summed + piece.astype(F32)]
    ppermute x1, waiting for transfers between devices: 1.6 us -> 3.62 us  [halos(): lax.ppermute(jnp.concatenate([go[:2], dec_pre[:1], ctrl_in[:1]], axis=0),...]
    unnamed x21, local copies, waits for them, and re-layouts: 2.91 us -> 4.26 us
  transfers between devices with their start and end apart: 18 -> 18, of which waited for: 9 -> 6; matrix products, arithmetic and copies ran while one was open for 6% -> 1% of each run, Pallas kernels for 9% -> 16%
where the time goes in v2:
time: 81.8 us; the launch traced here: 81.5 us
  starting transfers between devices  34.1 us (42%)
  Pallas kernels  23.4 us (29%)
  waiting for transfers between devices  15.9 us (19%)
  local copies, waits for them, and re-layouts  6.49 us (8%)
  between operations  1.04 us (1%)
    ppermute x14, starting transfers between devices, swap(): return lax.ppermute(values, axis, pairs)  24.5 us
    ppermute x14, waiting for transfers between devices, swap(): return lax.ppermute(values, axis, pairs)  12.3 us
    pallas_call x1, Pallas kernels, first(): pl.pallas_call(functools.partial(first_kernel, p), out_shape=(vm(((p.h +...  9.3 us
    pallas_call x1, Pallas kernels, second(): pl.pallas_call(functools.partial(second_kernel, p), out_shape=(slots, slo...  6.51 us
    ppermute x1, starting transfers between devices, halos(): left = lax.ppermute(own_r, 'col', forward)  4.55 us
    unnamed x21, local copies, waits for them, and re-layouts  4.26 us
    ppermute x1, waiting for transfers between devices, halos(): lax.ppermute(jnp.concatenate([go[:2], dec_pre[:1], ctrl_in[:1]], axis=0),...  3.62 us
    pallas_call x1, Pallas kernels, prep(): pl.pallas_call(functools.partial(prep_kernel, p), out_shape=(vm((p.np, 3...  3.39 us
  transfers between devices with their start and end apart: 18, of which 6 were waited for; matrix products, arithmetic and copies ran while one was open for 1% of the time, Pallas kernels for 16%

profile of v2, /device:TPU:0, one launch (start us, length us, event | category | flops | bytes accessed | tf_op | source)
XLA Modules:
  0.0 81.5 jit_solution(10714453881240234699)
XLA Ops:
  0.7 1.5 %copy.11 = bf16[32,32,320]{2,0,1:T(8,128)(2,1)S(1)} copy(bf16[32,32,320]{2,1,0:T(8,128)(2,1)} %go.1) | data formatting | bytes 1310720 | tf_op args[0]
  4.3 2.4 %collective-permute-start = (bf16[4,32,320]{2,0,1:T(4,128)(2,1)S(1)}, bf16[4,32,320]{2,0,1:T(4,128)(2,1)S(1)}, u32[]{:S(2)}, u32[]{:S(2)}) collective-permute-start(bf16[4,32,320]{2,0,1:T(4,128)(2,1)S(1)} %pad_maximum_fusion.2), channel_id=1, source_target_pairs={{0,4},{4,8},{8,12},{12,16},{16,20},{20,24},{24,28},{1,5},{5,9},{9,... | collective-permute-start | bytes 245768 | tf_op jit(solution)/shard_map/ppermute | solution.py:551
  8.7 3.6 %collective-permute-done.1 = bf16[4,32,320]{2,0,1:T(4,128)(2,1)S(1)} collective-permute-done((bf16[4,32,320]{2,0,1:T(4,128)(2,1)S(1)}, bf16[4,32,320]{2,0,1:T(4,128)(2,1)S(1)}, u32[]{:S(2)}, u32[]{:S(2)}) %collective-permute-start.1) | collective-permute-done | bytes 81952 | tf_op jit(solution)/shard_map/ppermute | solution.py:554
  12.6 1.3 %collective-permute-start.3 = (bf16[4,36,320]{2,1,0:T(8,128)(2,1)S(1)}, bf16[4,36,320]{2,1,0:T(8,128)(2,1)S(1)}, u32[]{:S(2)}, u32[]{:S(2)}) collective-permute-start(bf16[4,36,320]{2,1,0:T(8,128)(2,1)S(1)} %pad_maximum_fusion.1.own_l), channel_id=1, source_target_pairs={{1,0},{2,1},{3,2},{5,4},{6,5},{7,6},{9,8},{10,9},{11,10},{13,12},{... | collective-permute-start | bytes 276488 | tf_op jit(solution)/shard_map/ppermute | solution.py:576
  13.9 4.6 %collective-permute-start.2 = (bf16[4,36,320]{2,1,0:T(8,128)(2,1)S(1)}, bf16[4,36,320]{2,1,0:T(8,128)(2,1)S(1)}, u32[]{:S(2)}, u32[]{:S(2)}) collective-permute-start(bf16[4,36,320]{2,1,0:T(8,128)(2,1)S(1)} %pad_maximum_fusion.own_r), channel_id=1, source_target_pairs={{0,1},{1,2},{2,3},{4,5},{5,6},{6,7},{8,9},{9,10},{10,11},{12,13},{... | collective-permute-start | bytes 276488 | tf_op jit(solution)/shard_map/ppermute | solution.py:575
  18.5 1.6 %copy-done.4 = bf16[3,3,320,320]{3,2,1,0:T(8,128)(2,1)S(1)} copy-done((bf16[3,3,320,320]{3,2,1,0:T(8,128)(2,1)S(1)}, bf16[3,3,320,320]{3,2,1,0:T(8,128)(2,1)}, u32[]{:S(2)}) %copy-start.4) | copy-done | bytes 1843224
  21.1 3.4 %prep.1 = (bf16[512,3072]{1,0:T(8,128)(2,1)S(1)}, bf16[320,3072]{1,0:T(8,128)(2,1)S(1)}, bf16[512,512]{1,0:T(8,128)(2,1)S(1)}, bf16[320,1024]{1,0:T(8,128)(2,1)S...) custom-call(bf16[9,320,320]{2,1,0:T(8,128)(2,1)S(1)} %bitcast.46, ...), custom_call_target="tpu_custom_call" | custom-call | flops 2000000000 | bytes 20000000 | tf_op jit(solution)/shard_map/prep/pallas_call | solution.py:129
  24.6 9.3 %first.1 = (bf16[1088,1024]{1,0:T(8,128)(2,1)S(1)}, bf16[16,40,896]{2,1,0:T(8,128)(2,1)S(1)}, bf16[16,40,896]{2,1,0:T(8,128)(2,1)S(1)}) custom-call(bf16[32,32,320]{2,1,0:T(8,128)(2,1)S(1)} %copy-done, bf16[4,32,320]{2,1,0:T(8,128)(2,1)S(1)} %copy.22.top, bf16[4,32,320]{2,1,0:T(8,128)(2,1)S(1)} %copy.23.bottom, ...), custom_call_target="tpu_custom_call" | custom-call | flops 10000000000 | bytes 20000000 | tf_op jit(solution)/shard_map/first/pallas_call | solution.py:319
  33.9 2.7 %collective-permute-start.4 = (bf16[16,40,896]{2,1,0:T(8,128)(2,1)S(1)}, bf16[16,40,896]{2,1,0:T(8,128)(2,1)S(1)}, u32[]{:S(2)}, u32[]{:S(2)}) collective-permute-start(bf16[16,40,896]{2,1,0:T(8,128)(2,1)S(1)} %get-tuple-element.45), channel_id=1, source_target_pairs={{0,4},{4,0},{8,12},{12,8},{16,20},{20,16},{24,28},{28,24},{1,5},{5... | collective-permute-start | bytes 3440648 | tf_op jit(solution)/shard_map/onecore/ppermute | solution.py:392
  36.6 2.5 %act_columns.1.a_in = bf16[1088,1024]{1,0:T(8,128)(2,1)S(1)} custom-call(bf16[32,32,320]{2,1,0:T(8,128)(2,1)S(1)} %copy-done.2, bf16[4,32,320]{2,1,0:T(8,128)(2,1)S(1)} %copy.22.top, bf16[4,32,320]{2,1,0:T(8,128)(2,1)S(1)} %copy.23.bottom, bf16[4,36,320]{2,1,0:T(8,128)(2,1)S(1)} %collective-permute-done.2.left, ...), custom_call_target="tpu_custom_call" | custom-call | flops 1000000000 | bytes 4000000 | tf_op jit(solution)/shard_map/act_columns/pallas_call | solution.py:172
  39.1 6.5 %second.1 = (bf16[16,80,384]{2,1,0:T(8,128)(2,1)S(1)}, bf16[16,80,384]{2,1,0:T(8,128)(2,1)S(1)}) custom-call(bf16[1088,1024]{1,0:T(8,128)(2,1)S(1)} %get-tuple-element.58.g2, bf16[1088,1024]{1,0:T(8,128)(2,1)S(1)} %act_columns.1.a_in, bf16[320,3072]{1,0:T(8,128)(2,1)S(1)} %get-tuple-element.59.w2, f32[320,1024]{1,0:T(8,128)S(1)} %get-tuple-element.60.slope_t), custom_call_target="tpu_custom_call" | custom-call | flops 6000000000 | bytes 10000000 | tf_op jit(solution)/shard_map/second/pallas_call | solution.py:364
  46.0 1.8 %collective-permute-start.5 = (bf16[8,40,512]{2,1,0:T(8,128)(2,1)S(1)}, bf16[8,40,512]{2,1,0:T(8,128)(2,1)S(1)}, u32[]{:S(2)}, u32[]{:S(2)}) collective-permute-start(bf16[8,40,512]{2,1,0:T(8,128)(2,1)S(1)} %get-tuple-element.47), channel_id=1, source_target_pairs={{0,16},{4,20},{8,24},{12,28},{16,0},{20,4},{24,8},{28,12},{1,17},{... | collective-permute-start | bytes 983048 | tf_op jit(solution)/shard_map/one1a/ppermute | solution.py:392
  48.8 1.6 %collective-permute-start.14 = (bf16[8,40,384]{2,1,0:T(8,128)(2,1)S(1)}, bf16[8,40,384]{2,1,0:T(8,128)(2,1)S(1)}, u32[]{:S(2)}, u32[]{:S(2)}) collective-permute-start(bf16[8,40,384]{2,1,0:T(8,128)(2,1)S(1)} %get-tuple-element.68), channel_id=1, source_target_pairs={{0,1},{1,0},{2,3},{3,2},{4,5},{5,4},{6,7},{7,6},{8,9},{9,8},{10,11... | collective-permute-start | bytes 737288 | tf_op jit(solution)/shard_map/two1b/ppermute | solution.py:392
  50.4 2.5 %collective-permute-start.12 = (bf16[8,40,384]{2,1,0:T(8,128)(2,1)S(1)}, bf16[8,40,384]{2,1,0:T(8,128)(2,1)S(1)}, u32[]{:S(2)}, u32[]{:S(2)}) collective-permute-start(bf16[8,40,384]{2,1,0:T(8,128)(2,1)S(1)} %get-tuple-element.64), channel_id=1, source_target_pairs={{0,3},{1,2},{2,1},{3,0},{4,7},{5,6},{6,5},{7,4},{8,11},{9,10},{10,... | collective-permute-start | bytes 737288 | tf_op jit(solution)/shard_map/two1a/ppermute | solution.py:392
  52.9 3.3 %collective-permute-done.5.refs_1_ = bf16[8,40,512]{2,1,0:T(8,128)(2,1)S(1)} collective-permute-done((bf16[8,40,512]{2,1,0:T(8,128)(2,1)S(1)}, bf16[8,40,512]{2,1,0:T(8,128)(2,1)S(1)}, u32[]{:S(2)}, u32[]{:S(2)}) %collective-permute-start.5) | collective-permute-done | bytes 327712 | tf_op jit(solution)/shard_map/one1a/ppermute | solution.py:392
  56.2 2.5 %collective-permute-start.6 = (bf16[4,40,512]{2,1,0:T(8,128)(2,1)S(1)}, bf16[4,40,512]{2,1,0:T(8,128)(2,1)S(1)}, u32[]{:S(2)}, u32[]{:S(2)}) collective-permute-start(bf16[4,40,512]{2,1,0:T(8,128)(2,1)S(1)} %get-tuple-element.49), channel_id=1, source_target_pairs={{0,8},{4,12},{8,0},{12,4},{16,24},{20,28},{24,16},{28,20},{1,9},{5... | collective-permute-start | bytes 491528 | tf_op jit(solution)/shard_map/one2a/ppermute | solution.py:392
  59.1 1.8 %collective-permute-start.15 = (bf16[4,40,384]{2,1,0:T(8,128)(2,1)S(1)}, bf16[4,40,384]{2,1,0:T(8,128)(2,1)S(1)}, u32[]{:S(2)}, u32[]{:S(2)}) collective-permute-start(bf16[4,40,384]{2,1,0:T(8,128)(2,1)S(1)} %get-tuple-element.70), channel_id=1, source_target_pairs={{0,3},{1,2},{2,1},{3,0},{4,7},{5,6},{6,5},{7,4},{8,11},{9,10},{10,... | collective-permute-start | bytes 368648 | tf_op jit(solution)/shard_map/two2b/ppermute | solution.py:392
  60.9 4.2 %collective-permute-done.12.refs_1_ = bf16[8,40,384]{2,1,0:T(8,128)(2,1)S(1)} collective-permute-done((bf16[8,40,384]{2,1,0:T(8,128)(2,1)S(1)}, bf16[8,40,384]{2,1,0:T(8,128)(2,1)S(1)}, u32[]{:S(2)}, u32[]{:S(2)}) %collective-permute-start.12) | collective-permute-done | bytes 245792 | tf_op jit(solution)/shard_map/two1a/ppermute | solution.py:392
  65.3 4.0 %collective-permute-start.9 = (bf16[2,40,896]{2,1,0:T(8,128)(2,1)S(1)}, bf16[2,40,896]{2,1,0:T(8,128)(2,1)S(1)}, u32[]{:S(2)}, u32[]{:S(2)}) collective-permute-start(bf16[2,40,896]{2,1,0:T(8,128)(2,1)S(1)} %get-tuple-element.55), channel_id=1, source_target_pairs={{0,3},{1,2},{2,1},{3,0},{4,7},{5,6},{6,5},{7,4},{8,11},{9,10},{10,... | collective-permute-start | bytes 430088 | tf_op jit(solution)/shard_map/one3a/ppermute | solution.py:392
  69.3 1.9 %collective-permute-done.13.refs_1_ = bf16[4,40,384]{2,1,0:T(8,128)(2,1)S(1)} collective-permute-done((bf16[4,40,384]{2,1,0:T(8,128)(2,1)S(1)}, bf16[4,40,384]{2,1,0:T(8,128)(2,1)S(1)}, u32[]{:S(2)}, u32[]{:S(2)}) %collective-permute-start.13) | collective-permute-done | bytes 122912 | tf_op jit(solution)/shard_map/two2a/ppermute | solution.py:392
  71.2 1.7 %collective-permute-start.16 = (bf16[2,80,384]{2,1,0:T(8,128)(2,1)S(1)}, bf16[2,80,384]{2,1,0:T(8,128)(2,1)S(1)}, u32[]{:S(2)}, u32[]{:S(2)}) collective-permute-start(bf16[2,80,384]{2,1,0:T(8,128)(2,1)S(1)} %get-tuple-element.72), channel_id=1, source_target_pairs={{0,16},{4,20},{8,24},{12,28},{16,0},{20,4},{24,8},{28,12},{1,17},{... | collective-permute-start | bytes 368648 | tf_op jit(solution)/shard_map/two3a/ppermute | solution.py:392
  73.7 2.6 %collective-permute-start.10 = (bf16[1,40,896]{2,1,0:T(8,128)(2,1)S(1)}, bf16[1,40,896]{2,1,0:T(8,128)(2,1)S(1)}, u32[]{:S(2)}, u32[]{:S(2)}) collective-permute-start(bf16[1,40,896]{2,1,0:T(8,128)(2,1)S(1)} %get-tuple-element.57), channel_id=1, source_target_pairs={{0,1},{1,0},{2,3},{3,2},{4,5},{5,4},{6,7},{7,6},{8,9},{9,8},{10,11... | collective-permute-start | bytes 215048 | tf_op jit(solution)/shard_map/one4a/ppermute | solution.py:392
  76.3 2.1 %collective-permute-start.17 = (bf16[1,80,384]{2,1,0:T(8,128)(2,1)S(1)}, bf16[1,80,384]{2,1,0:T(8,128)(2,1)S(1)}, u32[]{:S(2)}, u32[]{:S(2)}) collective-permute-start(bf16[1,80,384]{2,1,0:T(8,128)(2,1)S(1)} %get-tuple-element.74), channel_id=1, source_target_pairs={{0,8},{4,12},{8,0},{12,4},{16,24},{20,28},{24,16},{28,20},{1,9},{5... | collective-permute-start | bytes 184328 | tf_op jit(solution)/shard_map/two4a/ppermute | solution.py:392
  78.5 2.2 %collective-permute-done.17.got2 = bf16[1,80,384]{2,1,0:T(8,128)(2,1)S(1)} collective-permute-done((bf16[1,80,384]{2,1,0:T(8,128)(2,1)S(1)}, bf16[1,80,384]{2,1,0:T(8,128)(2,1)S(1)}, u32[]{:S(2)}, u32[]{:S(2)}) %collective-permute-start.17) | collective-permute-done | bytes 61472 | tf_op jit(solution)/shard_map/two4a/ppermute | solution.py:392
  (69 shorter events, 8.9 us)
Async XLA Ops:
  0.6 7.7 %copy-start.1 = (bf16[32,32,320]{2,1,0:T(8,128)(2,1)S(1)}, bf16[32,32,320]{2,1,0:T(8,128)(2,1)}, u32[]{:S(2)}) copy-start(bf16[32,32,320]{2,1,0:T(8,128)(2,1)} %param.9) | copy-start | bytes 1966084
  0.6 7.8 %copy-start.2 = (bf16[32,32,320]{2,1,0:T(8,128)(2,1)S(1)}, bf16[32,32,320]{2,1,0:T(8,128)(2,1)}, u32[]{:S(2)}) copy-start(bf16[32,32,320]{2,1,0:T(8,128)(2,1)} %x_ref.1) | copy-start | bytes 1966084
  2.2 16.3 %copy-start.3 = (bf16[3,3,320,320]{3,2,1,0:T(8,128)(2,1)S(1)}, bf16[3,3,320,320]{3,2,1,0:T(8,128)(2,1)}, u32[]{:S(2)}) copy-start(bf16[3,3,320,320]{3,2,1,0:T(8,128)(2,1)} %param.13) | copy-start | bytes 5529604
  2.2 16.3 %copy-start.5 = (bf16[32,32,320]{2,1,0:T(8,128)(2,1)S(1)}, bf16[32,32,320]{2,1,0:T(8,128)(2,1)}, u32[]{:S(2)}) copy-start(bf16[32,32,320]{2,1,0:T(8,128)(2,1)} %param.11) | copy-start | bytes 1966084
  2.2 16.3 %copy-start.6 = (bf16[32,32,320]{2,1,0:T(8,128)(2,1)S(1)}, bf16[32,32,320]{2,1,0:T(8,128)(2,1)}, u32[]{:S(2)}) copy-start(bf16[32,32,320]{2,1,0:T(8,128)(2,1)} %param.10) | copy-start | bytes 1966084
  4.3 4.3 %collective-permute-start = (bf16[4,32,320]{2,0,1:T(4,128)(2,1)S(1)}, bf16[4,32,320]{2,0,1:T(4,128)(2,1)S(1)}, u32[]{:S(2)}, u32[]{:S(2)}) collective-permute-start(bf16[4,32,320]{2,0,1:T(4,128)(2,1)S(1)} %pad_maximum_fusion.2), channel_id=1, source_target_pairs={{0,4},{4,8},{8,12},{12,16},{16,20},{20,24},{24,28},{1,5},{5,9},{9,... | collective-permute-start | bytes 245768 | tf_op jit(solution)/shard_map/ppermute | solution.py:551
  7.0 5.3 %collective-permute-start.1 = (bf16[4,32,320]{2,0,1:T(4,128)(2,1)S(1)}, bf16[4,32,320]{2,0,1:T(4,128)(2,1)S(1)}, u32[]{:S(2)}, u32[]{:S(2)}) collective-permute-start(bf16[4,32,320]{2,0,1:T(4,128)(2,1)S(1)} %pad_maximum_fusion.3), channel_id=1, source_target_pairs={{4,0},{8,4},{12,8},{16,12},{20,16},{24,20},{28,24},{5,1},{9,5},{13... | collective-permute-start | bytes 245768 | tf_op jit(solution)/shard_map/ppermute | solution.py:554
  12.6 12.0 %collective-permute-start.3 = (bf16[4,36,320]{2,1,0:T(8,128)(2,1)S(1)}, bf16[4,36,320]{2,1,0:T(8,128)(2,1)S(1)}, u32[]{:S(2)}, u32[]{:S(2)}) collective-permute-start(bf16[4,36,320]{2,1,0:T(8,128)(2,1)S(1)} %pad_maximum_fusion.1.own_l), channel_id=1, source_target_pairs={{1,0},{2,1},{3,2},{5,4},{6,5},{7,6},{9,8},{10,9},{11,10},{13,12},{... | collective-permute-start | bytes 276488 | tf_op jit(solution)/shard_map/ppermute | solution.py:576
  13.9 10.6 %collective-permute-start.2 = (bf16[4,36,320]{2,1,0:T(8,128)(2,1)S(1)}, bf16[4,36,320]{2,1,0:T(8,128)(2,1)S(1)}, u32[]{:S(2)}, u32[]{:S(2)}) collective-permute-start(bf16[4,36,320]{2,1,0:T(8,128)(2,1)S(1)} %pad_maximum_fusion.own_r), channel_id=1, source_target_pairs={{0,1},{1,2},{2,3},{4,5},{5,6},{6,7},{8,9},{9,10},{10,11},{12,13},{... | collective-permute-start | bytes 276488 | tf_op jit(solution)/shard_map/ppermute | solution.py:575
  21.1 3.5 %copy-start = (bf16[32,32,320]{2,1,0:T(8,128)(2,1)S(1)}, bf16[32,32,320]{2,1,0:T(8,128)(2,1)}, u32[]{:S(2)}) copy-start(bf16[32,32,320]{2,1,0:T(8,128)(2,1)} %go.1) | copy-start | bytes 1966084
  33.9 11.9 %collective-permute-start.4 = (bf16[16,40,896]{2,1,0:T(8,128)(2,1)S(1)}, bf16[16,40,896]{2,1,0:T(8,128)(2,1)S(1)}, u32[]{:S(2)}, u32[]{:S(2)}) collective-permute-start(bf16[16,40,896]{2,1,0:T(8,128)(2,1)S(1)} %get-tuple-element.45), channel_id=1, source_target_pairs={{0,4},{4,0},{8,12},{12,8},{16,20},{20,16},{24,28},{28,24},{1,5},{5... | collective-permute-start | bytes 3440648 | tf_op jit(solution)/shard_map/onecore/ppermute | solution.py:392
  45.7 2.9 %collective-permute-start.11 = (bf16[16,80,384]{2,1,0:T(8,128)(2,1)S(1)}, bf16[16,80,384]{2,1,0:T(8,128)(2,1)S(1)}, u32[]{:S(2)}, u32[]{:S(2)}) collective-permute-start(bf16[16,80,384]{2,1,0:T(8,128)(2,1)S(1)} %get-tuple-element.62), channel_id=1, source_target_pairs={{0,4},{4,0},{8,12},{12,8},{16,20},{20,16},{24,28},{28,24},{1,5},{5... | collective-permute-start | bytes 2949128 | tf_op jit(solution)/shard_map/twocore/ppermute | solution.py:392
  46.0 10.2 %collective-permute-start.5 = (bf16[8,40,512]{2,1,0:T(8,128)(2,1)S(1)}, bf16[8,40,512]{2,1,0:T(8,128)(2,1)S(1)}, u32[]{:S(2)}, u32[]{:S(2)}) collective-permute-start(bf16[8,40,512]{2,1,0:T(8,128)(2,1)S(1)} %get-tuple-element.47), channel_id=1, source_target_pairs={{0,16},{4,20},{8,24},{12,28},{16,0},{20,4},{24,8},{28,12},{1,17},{... | collective-permute-start | bytes 983048 | tf_op jit(solution)/shard_map/one1a/ppermute | solution.py:392
  47.8 10.8 %collective-permute-start.7 = (bf16[8,40,384]{2,1,0:T(8,128)(2,1)S(1)}, bf16[8,40,384]{2,1,0:T(8,128)(2,1)S(1)}, u32[]{:S(2)}, u32[]{:S(2)}) collective-permute-start(bf16[8,40,384]{2,1,0:T(8,128)(2,1)S(1)} %get-tuple-element.51), channel_id=1, source_target_pairs={{0,8},{4,12},{8,0},{12,4},{16,24},{20,28},{24,16},{28,20},{1,9},{5... | collective-permute-start | bytes 737288 | tf_op jit(solution)/shard_map/one1b/ppermute | solution.py:392
  48.8 10.3 %collective-permute-start.14 = (bf16[8,40,384]{2,1,0:T(8,128)(2,1)S(1)}, bf16[8,40,384]{2,1,0:T(8,128)(2,1)S(1)}, u32[]{:S(2)}, u32[]{:S(2)}) collective-permute-start(bf16[8,40,384]{2,1,0:T(8,128)(2,1)S(1)} %get-tuple-element.68), channel_id=1, source_target_pairs={{0,1},{1,0},{2,3},{3,2},{4,5},{5,4},{6,7},{7,6},{8,9},{9,8},{10,11... | collective-permute-start | bytes 737288 | tf_op jit(solution)/shard_map/two1b/ppermute | solution.py:392
  50.4 14.6 %collective-permute-start.12 = (bf16[8,40,384]{2,1,0:T(8,128)(2,1)S(1)}, bf16[8,40,384]{2,1,0:T(8,128)(2,1)S(1)}, u32[]{:S(2)}, u32[]{:S(2)}) collective-permute-start(bf16[8,40,384]{2,1,0:T(8,128)(2,1)S(1)} %get-tuple-element.64), channel_id=1, source_target_pairs={{0,3},{1,2},{2,1},{3,0},{4,7},{5,6},{6,5},{7,4},{8,11},{9,10},{10,... | collective-permute-start | bytes 737288 | tf_op jit(solution)/shard_map/two1a/ppermute | solution.py:392
  56.2 9.0 %collective-permute-start.6 = (bf16[4,40,512]{2,1,0:T(8,128)(2,1)S(1)}, bf16[4,40,512]{2,1,0:T(8,128)(2,1)S(1)}, u32[]{:S(2)}, u32[]{:S(2)}) collective-permute-start(bf16[4,40,512]{2,1,0:T(8,128)(2,1)S(1)} %get-tuple-element.49), channel_id=1, source_target_pairs={{0,8},{4,12},{8,0},{12,4},{16,24},{20,28},{24,16},{28,20},{1,9},{5... | collective-permute-start | bytes 491528 | tf_op jit(solution)/shard_map/one2a/ppermute | solution.py:392
  58.7 6.4 %collective-permute-start.8 = (bf16[4,40,384]{2,1,0:T(8,128)(2,1)S(1)}, bf16[4,40,384]{2,1,0:T(8,128)(2,1)S(1)}, u32[]{:S(2)}, u32[]{:S(2)}) collective-permute-start(bf16[4,40,384]{2,1,0:T(8,128)(2,1)S(1)} %get-tuple-element.53), channel_id=1, source_target_pairs={{0,16},{4,20},{8,24},{12,28},{16,0},{20,4},{24,8},{28,12},{1,17},{... | collective-permute-start | bytes 368648 | tf_op jit(solution)/shard_map/one2b/ppermute | solution.py:392
  59.1 10.1 %collective-permute-start.15 = (bf16[4,40,384]{2,1,0:T(8,128)(2,1)S(1)}, bf16[4,40,384]{2,1,0:T(8,128)(2,1)S(1)}, u32[]{:S(2)}, u32[]{:S(2)}) collective-permute-start(bf16[4,40,384]{2,1,0:T(8,128)(2,1)S(1)} %get-tuple-element.70), channel_id=1, source_target_pairs={{0,3},{1,2},{2,1},{3,0},{4,7},{5,6},{6,5},{7,4},{8,11},{9,10},{10,... | collective-permute-start | bytes 368648 | tf_op jit(solution)/shard_map/two2b/ppermute | solution.py:392
  65.1 6.1 %collective-permute-start.13 = (bf16[4,40,384]{2,1,0:T(8,128)(2,1)S(1)}, bf16[4,40,384]{2,1,0:T(8,128)(2,1)S(1)}, u32[]{:S(2)}, u32[]{:S(2)}) collective-permute-start(bf16[4,40,384]{2,1,0:T(8,128)(2,1)S(1)} %get-tuple-element.66), channel_id=1, source_target_pairs={{0,1},{1,0},{2,3},{3,2},{4,5},{5,4},{6,7},{7,6},{8,9},{9,8},{10,11... | collective-permute-start | bytes 368648 | tf_op jit(solution)/shard_map/two2a/ppermute | solution.py:392
  65.3 8.4 %collective-permute-start.9 = (bf16[2,40,896]{2,1,0:T(8,128)(2,1)S(1)}, bf16[2,40,896]{2,1,0:T(8,128)(2,1)S(1)}, u32[]{:S(2)}, u32[]{:S(2)}) collective-permute-start(bf16[2,40,896]{2,1,0:T(8,128)(2,1)S(1)} %get-tuple-element.55), channel_id=1, source_target_pairs={{0,3},{1,2},{2,1},{3,0},{4,7},{5,6},{6,5},{7,4},{8,11},{9,10},{10,... | collective-permute-start | bytes 430088 | tf_op jit(solution)/shard_map/one3a/ppermute | solution.py:392
  71.2 5.1 %collective-permute-start.16 = (bf16[2,80,384]{2,1,0:T(8,128)(2,1)S(1)}, bf16[2,80,384]{2,1,0:T(8,128)(2,1)S(1)}, u32[]{:S(2)}, u32[]{:S(2)}) collective-permute-start(bf16[2,80,384]{2,1,0:T(8,128)(2,1)S(1)} %get-tuple-element.72), channel_id=1, source_target_pairs={{0,16},{4,20},{8,24},{12,28},{16,0},{20,4},{24,8},{28,12},{1,17},{... | collective-permute-start | bytes 368648 | tf_op jit(solution)/shard_map/two3a/ppermute | solution.py:392
  73.7 7.0 %collective-permute-start.10 = (bf16[1,40,896]{2,1,0:T(8,128)(2,1)S(1)}, bf16[1,40,896]{2,1,0:T(8,128)(2,1)S(1)}, u32[]{:S(2)}, u32[]{:S(2)}) collective-permute-start(bf16[1,40,896]{2,1,0:T(8,128)(2,1)S(1)} %get-tuple-element.57), channel_id=1, source_target_pairs={{0,1},{1,0},{2,3},{3,2},{4,5},{5,4},{6,7},{7,6},{8,9},{9,8},{10,11... | collective-permute-start | bytes 215048 | tf_op jit(solution)/shard_map/one4a/ppermute | solution.py:392
  76.3 4.3 %collective-permute-start.17 = (bf16[1,80,384]{2,1,0:T(8,128)(2,1)S(1)}, bf16[1,80,384]{2,1,0:T(8,128)(2,1)S(1)}, u32[]{:S(2)}, u32[]{:S(2)}) collective-permute-start(bf16[1,80,384]{2,1,0:T(8,128)(2,1)S(1)} %get-tuple-element.74), channel_id=1, source_target_pairs={{0,8},{4,12},{8,0},{12,4},{16,24},{20,28},{24,16},{28,20},{1,9},{5... | collective-permute-start | bytes 184328 | tf_op jit(solution)/shard_map/two4a/ppermute | solution.py:392
  (2 other events, 2.6 us)
